TPU v7x, 256 devices: a whole 4x4x8 slice. The times are simulated.
256 devices in a mesh: dp: 8 (over y, x_hi), tok: 16 (over z, core), col: 2 (over x_lo).
Axes of the slice: x: 4 (x_hi: 2, x_lo: 2; x = x_hi * 2 + x_lo), y: 4, z: 8, core: 2. Of those that a mesh axis runs over, the one named last changes fastest.
Arguments:
- tokens: bfloat16 [8, 8192, 1024], P('dp', 'tok'), may hold values from -6 to 6
- ln_gain: bfloat16 [1024], replicated, may hold values from 0.099609375 to 1.8984375
- qkv_weight: bfloat16 [3, 1024, 512], P(None, None, 'col'), may hold values from -0.375 to 0.375
- out_weight: bfloat16 [512, 1024], P('col'), may hold values from -0.25 to 0.25
- readout_weight: bfloat16 [1024, 64], replicated, may hold values from -0.1875 to 0.1875
- conv_weight: bfloat16 [2, 64, 576], replicated, may hold values from -0.25 to 0.25
- head_weight: bfloat16 [2, 64], replicated, may hold values from -0.75 to 0.75
- holo_cot: float32 [8, 2, 32, 256], P('dp', None, 'tok', 'col'), may hold values from -1 to 1
Outputs:
- hologram: float32 [8, 2, 32, 256], P('dp', None, 'tok', 'col')
- conv_grad: float32 [2, 64, 576], replicated
- out_grad: float32 [512, 1024], P('col')
All inputs are finite; a program needn't handle non-finite values.
Results may differ from a plain program's by a relative error of at most 0.017.
The roundings to bfloat16 on the way count: a program that leaves them out, or rounds other values in their place, can miss the bound.
Values may be sent and summed in bfloat16 or wider, within the bound.
A program may use at most 128 MiB of HBM per device.

v0:
```python
import jax
import jax.numpy as jnp
from jax import lax
from jax.sharding import PartitionSpec as P

HEAD = 64


EPSILON = 1e-05


def extended(shard, sides, width):
    for axis, dim in sides:
        size, length = (lax.axis_size(axis), shard.shape[dim])
        up = [(i, (i + 1) % size) for i in range(size - 1)]
        down = [(j, i) for i, j in up]
        last = lax.slice_in_dim(shard, length - width, length, axis=dim)
        initial = lax.slice_in_dim(shard, 0, width, axis=dim)
        before = lax.ppermute(last, axis, up)
        after = lax.ppermute(initial, axis, down)
        shard = jnp.concatenate([before, shard, after], axis=dim)
    return shard


def joined_along(blocks, dim):
    shape = list(blocks.shape[1:])
    shape[dim] *= blocks.shape[0]
    return jnp.moveaxis(blocks, 0, dim).reshape(shape)


def copy_for_each(shard, axis):
    size = lax.axis_size(axis)
    return lax.all_to_all(
        jnp.broadcast_to(shard[None], (size, *shard.shape)), axis, 0, 0, tiled=True
    )


def gather_directly(shard, axis, dim):
    return joined_along(copy_for_each(shard, axis), dim)


def sent_together(arrays, axis, dim, along):
    ends, at = ([], 0)
    for a in arrays[:-1]:
        at += a.shape[along]
        ends.append(at)
    both = jnp.concatenate(arrays, axis=along)
    return tuple(jnp.split(lax.all_gather(both, axis, axis=dim, tiled=True), ends, axis=along))


def normalize(rows_in, ln_gain):
    values = rows_in.astype(jnp.float32)
    center = values - jnp.mean(values, axis=-1, keepdims=True)
    spread = jnp.mean(center * center, axis=-1, keepdims=True)
    return (center * lax.rsqrt(spread + EPSILON) * ln_gain.astype(jnp.float32)).astype(jnp.bfloat16)


def project(normed, weights_all):
    return tuple(
        (
            jnp.dot(normed, weights_all[member], preferred_element_type=jnp.float32).astype(
                jnp.bfloat16
            )
            for member in range(3)
        )
    )


def empty_state(queries):
    query_count = queries.shape[0]
    head_count = queries.shape[1] // HEAD
    return (
        jnp.zeros((query_count, head_count, HEAD), jnp.float32),
        jnp.full((head_count, query_count), -1e30, jnp.float32),
        jnp.zeros((head_count, query_count), jnp.float32),
    )


def absorb(queries, running, key_rows, value_rows):
    summed, row_top, row_total = running
    head_count = summed.shape[1]
    query_view = queries.reshape(queries.shape[0], head_count, HEAD)
    key_view = key_rows.reshape(key_rows.shape[0], head_count, HEAD)
    value_view = value_rows.reshape(value_rows.shape[0], head_count, HEAD)
    scores = jnp.einsum(
        "qhd,khd->hqk", query_view, key_view, preferred_element_type=jnp.float32
    ) * (1.0 / HEAD**0.5)
    new_top = jnp.maximum(row_top, jnp.max(scores, axis=-1))
    rescale = jnp.exp(row_top - new_top)
    raised = jnp.exp(scores - new_top[:, :, None])
    row_total = row_total * rescale + jnp.sum(raised, axis=-1)
    weighted = jnp.einsum(
        "hqk,khd->qhd", raised.astype(jnp.bfloat16), value_view, preferred_element_type=jnp.float32
    )
    summed = summed * jnp.transpose(rescale)[:, :, None] + weighted
    return (summed, new_top, row_total)


def absorb_keys(queries, running, arrived):
    key_rows, value_rows = arrived
    total_rows = key_rows.shape[0]
    block_rows = 512
    block_count = total_rows // block_rows

    def advance(turn_at, carried):
        key_block = lax.dynamic_slice_in_dim(key_rows, turn_at * block_rows, block_rows, 0)
        value_block = lax.dynamic_slice_in_dim(value_rows, turn_at * block_rows, block_rows, 0)
        return absorb(queries, carried, key_block, value_block)

    return lax.fori_loop(0, block_count, advance, running)


def finish(running):
    summed, row_top, row_total = running
    return (
        (summed / jnp.transpose(row_total)[:, :, None])
        .reshape(summed.shape[0], -1)
        .astype(jnp.bfloat16)
    )


def neighbourhood(padded, grid_rows, grid_cols):
    pieces = [
        padded[:, row_off : row_off + grid_rows, col_off : col_off + grid_cols]
        for row_off in range(3)
        for col_off in range(3)
    ]
    return jnp.concatenate(pieces, axis=0).reshape(9 * padded.shape[0], grid_rows * grid_cols)


def flipped(padded, grid_rows, grid_cols):
    pieces = [
        padded[:, 2 - row_off : 2 - row_off + grid_rows, 2 - col_off : 2 - col_off + grid_cols]
        for row_off in range(3)
        for col_off in range(3)
    ]
    return jnp.concatenate(pieces, axis=0).reshape(9 * padded.shape[0], grid_rows * grid_cols)


def transposed(weight):
    channels = weight.shape[0]
    return jnp.transpose(weight.reshape(channels, 9, channels), (2, 1, 0)).reshape(
        channels, 9 * channels
    )


def with_rims(field):
    return extended(field, (("tok", 1), ("col", 2)), 1)


def shards(
    tokens, ln_gain, qkv_weight, out_weight, readout_weight, conv_weight, head_weight, holo_cot
):
    frame_rows = tokens[0]
    cotangent = holo_cot[0]
    rows_dev = cotangent.shape[1]
    cols_dev = cotangent.shape[2]
    col_count = lax.axis_size("col")
    col_at = lax.axis_index("col")
    channels = conv_weight.shape[1]
    layer_count = conv_weight.shape[0]
    width = frame_rows.shape[1]
    own_rows = lax.dynamic_index_in_dim(
        frame_rows.reshape(rows_dev, col_count, cols_dev, width), col_at, 1, keepdims=False
    ).reshape(rows_dev * cols_dev, width)
    own_values = own_rows.astype(jnp.float32)
    readout_wide = readout_weight.astype(jnp.float32)
    readout_back = jnp.transpose(readout_wide)
    all_projections = lax.all_gather(qkv_weight, "col", axis=2, tiled=True)
    all_outputs = gather_directly(out_weight, "col", 0)
    normed = normalize(own_rows, ln_gain)
    queries, key_rows, value_rows = project(normed, all_projections)
    running = absorb_keys(
        queries, empty_state(queries), sent_together((key_rows, value_rows), ("tok", "col"), 0, 1)
    )
    context = finish(running)
    mixed = own_values + jnp.dot(context, all_outputs, preferred_element_type=jnp.float32)
    readout = jnp.dot(mixed, readout_wide, precision=lax.Precision.HIGHEST)
    hidden = jnp.transpose(readout.astype(jnp.bfloat16)).reshape(channels, rows_dev, cols_dev)
    inputs = []
    pre_acts = []
    for layer_at in range(layer_count):
        stacked = neighbourhood(with_rims(hidden), rows_dev, cols_dev)
        pre_act = jnp.dot(conv_weight[layer_at], stacked, preferred_element_type=jnp.float32)
        inputs.append(stacked)
        pre_acts.append(pre_act)
        hidden = jax.nn.silu(pre_act).astype(jnp.bfloat16).reshape(channels, rows_dev, cols_dev)
    hologram = jnp.dot(
        head_weight, hidden.reshape(channels, -1), preferred_element_type=jnp.float32
    )
    grad_hidden = jnp.dot(
        jnp.transpose(head_weight.astype(jnp.float32)),
        cotangent.reshape(cotangent.shape[0], -1),
        precision=lax.Precision.HIGHEST,
    ).astype(jnp.bfloat16)
    conv_terms = [None] * layer_count
    for layer_at in reversed(range(layer_count)):
        pre_act = pre_acts[layer_at]
        sigmoid_pre = jax.nn.sigmoid(pre_act)
        grad_pre = (
            grad_hidden.astype(jnp.float32) * sigmoid_pre * (1.0 + pre_act * (1.0 - sigmoid_pre))
        ).astype(jnp.bfloat16)
        conv_terms[layer_at] = lax.dot_general(
            grad_pre, inputs[layer_at], (((1,), (1,)), ((), ())), preferred_element_type=jnp.float32
        )
        padded = with_rims(grad_pre.reshape(channels, rows_dev, cols_dev))
        grad_hidden = jnp.dot(
            transposed(conv_weight[layer_at]),
            flipped(padded, rows_dev, cols_dev),
            preferred_element_type=jnp.float32,
        ).astype(jnp.bfloat16)
    conv_grad = lax.psum(jnp.stack(conv_terms), ("dp", "tok", "col"))
    shard_rows = out_weight.shape[0]
    small_term = lax.dot_general(
        context, grad_hidden, (((0,), (1,)), ((), ())), preferred_element_type=jnp.float32
    )
    grad_small = lax.psum(small_term, ("dp", "tok", "col"))
    own_small = lax.dynamic_slice_in_dim(grad_small, col_at * shard_rows, shard_rows, 0)
    out_grad = jnp.dot(own_small, readout_back, precision=lax.Precision.HIGHEST)
    return (hologram.reshape(1, cotangent.shape[0], rows_dev, cols_dev), conv_grad, out_grad)


def solution(mesh):
    in_specs = (
        P("dp", "tok", None),
        P(),
        P(None, None, "col"),
        P("col", None),
        P(),
        P(),
        P(),
        P("dp", None, "tok", "col"),
    )
    out_specs = (P("dp", None, "tok", "col"), P(), P("col", None))
    return jax.shard_map(shards, mesh=mesh, in_specs=in_specs, out_specs=out_specs, check_vma=False)
```

profile of v0, /device:TPU:1, one launch (start us, length us, event | category | flops | bytes accessed | tf_op | source)
XLA Modules:
  0.0 608.6 jit_solution(3435451693195484029)
XLA Ops:
  9.9 1.3 multiply_reduce_fusion
  11.2 1.3 multiply_convert_fusion
  12.6 50.8 %all-gather.3.cloned.1.call-done = bf16[3,1024,512]{2,1,0:T(8,128)(2,1)} async-done(((bf16[3,1024,256]{2,1,0:T(8,128)(2,1)}), bf16[3,1024,512]{2,1,0:T(8,128)(2,1)}) %all-gather.3.cloned.1.call-update) | async-done | bytes 3145744 | tf_op jit(solution)/shard_map/all_gather | solution.py:169
  63.4 1.7 convolution_convert_fusion.1
  65.1 1.7 convolution_convert_fusion.2
  68.8 3.6 all-to-all-start
  73.6 1.7 convolution_convert_fusion
  75.4 107.3 %all-gather.5.cloned.1.call-done = bf16[8192,1024]{1,0:T(8,128)(2,1)} async-done(((bf16[256,1024]{1,0:T(8,128)(2,1)}), bf16[8192,1024]{1,0:T(8,128)(2,1)}) %all-gather.5.cloned.1.call-update) | async-done | bytes 16777232 | tf_op jit(solution)/shard_map/all_gather | solution.py:48
  182.7 11.3 %fusion.37 = (bf16[8192,512]{1,0:T(8,128)(2,1)}, bf16[8192,512]{1,0:T(8,128)(2,1)}) fusion(bf16[8192,1024]{1,0:T(8,128)(2,1)} %all-gather.5.cloned.1.call-done), kind=kLoop, calls=%fused_computation.157 | loop fusion | bytes 33554432 | tf_op jit(solution)/shard_map/split | solution.py:48
  194.1 67.4 %while.18 = (s32[]{:T(128)}, f32[256,8,64]{0,2,1:T(8,128)S(1)}, f32[8,256]{1,0:T(8,128)S(1)}, f32[8,256]{1,0:T(8,128)S(1)}, bf16[8192,512]{1,0:T(8,128)(2,1)}, /...) while((s32[]{:T(128)}, f32[256,8,64]{0,2,1:T(8,128)S(1)}, ...), condition=%wide.region_5.6_spmd.clone, body=%wide.region_2.5_spmd.clone.sunk | while | flops 277229568 | bytes 19267760 | solution.py:110
  261.6 1.7 convolution_add_fusion
  264.1 5.3 collective-permute-start
  269.4 1.9 collective-permute-start.1
  271.3 3.3 collective-permute-done.1
  274.8 2.0 collective-permute-start.2
  278.8 3.1 collective-permute-done.3
  283.1 4.1 collective-permute-start.4
  287.2 1.9 collective-permute-start.5
  289.1 3.3 collective-permute-done.5
  292.6 1.3 collective-permute-start.6
  295.9 3.1 collective-permute-done.7
  300.4 4.1 collective-permute-start.8
  304.5 1.9 collective-permute-start.9
  307.0 2.7 collective-permute-done.9
  311.4 4.2 collective-permute-start.11
  317.9 3.9 collective-permute-start.12
  321.9 1.9 collective-permute-start.13
  324.0 3.3 collective-permute-done.13
  329.6 4.0 collective-permute-start.15
  337.7 260.2 %all-reduce.3.cloned.1.call-done = (f32[2,64,576]{2,1,0:T(8,128)}, f32[512,64]{1,0:T(8,128)}) async-done(((f32[2,64,576]{2,1,0:T(8,128)}, f32[512,64]{1,0:T(8,128)}), (f32[2,64,576]{2,1,0:T(8,128)}, f32[512,64]{1,0:T(8,128)})) %all-reduce.3.cloned.1.call-update) | async-done | bytes 426000 | tf_op jit(solution)/shard_map/psum | solution.py:212
  597.9 2.4 fusion.27
  600.3 1.7 copy.147
  (265 shorter events, 90.9 us)
Async XLA Ops:
  7.2 256.1 %copy-start = (bf16[1024,64]{0,1:T(8,128)(2,1)S(1)}, bf16[1024,64]{0,1:T(8,128)(2,1)}, u32[]{:S(2)}) copy-start(bf16[1024,64]{0,1:T(8,128)(2,1)} %param.14) | copy-start | bytes 393220
  7.2 56.2 %all-gather.3.cloned.1.call-start = ((), (), s32[]{:S(2)}) async-start(), calls=%async_computation.1 | async-start | bytes 4718592 | tf_op jit(solution)/shard_map/all_gather | solution.py:169
  7.9 59.8 %copy-start.2 = (bf16[256,1024]{1,0:T(8,128)(2,1)S(1)}, bf16[256,1024]{1,0:T(8,128)(2,1)}, u32[]{:S(2)}) copy-start(bf16[256,1024]{1,0:T(8,128)(2,1)} %param.13) | copy-start | bytes 1572868
  7.9 174.8 %all-gather.5.cloned.1.call-start = ((), (), s32[]{:S(2)}) async-start(), calls=%async_computation.2 | async-start | bytes 17301504 | tf_op jit(solution)/shard_map/all_gather | solution.py:48
  65.0 7.5 %copy-start.1 = (bf16[1,512,1024]{2,1,0:T(8,128)(2,1)S(1)}, bf16[1,512,1024]{2,1,0:T(8,128)(2,1)}, u32[]{:S(2)}) copy-start(bf16[1,512,1024]{2,1,0:T(8,128)(2,1)} %param.10) | copy-start | bytes 3145732
  68.8 192.7 %all-to-all-start = ((bf16[2,256,1024]{2,1,0:T(8,128)(2,1)}), bf16[2,256,1024]{2,1,0:T(8,128)(2,1)S(1)}, u32[]{:S(2)}, u32[]{:S(2)}) async-start(bf16[2,256,1024]{2,1,0:T(8,128)(2,1)} %broadcast_in_dim.28), calls=%async_computation | async-start | bytes 2097152 | tf_op jit(solution)/shard_map/all_to_all | solution.py:33
  72.4 525.5 %all-reduce.3.cloned.1.call-start = ((), (), s32[]{:S(2)}) async-start(), calls=%async_computation.3 | async-start | bytes 1179648 | tf_op jit(solution)/shard_map/psum | solution.py:212
  261.5 21.3 %copy-start.3 = (bf16[2,64,576]{2,1,0:T(8,128)(2,1)S(1)}, bf16[2,64,576]{2,1,0:T(8,128)(2,1)}, u32[]{:S(2)}) copy-start(bf16[2,64,576]{2,1,0:T(8,128)(2,1)} %param.15) | copy-start | bytes 442372
  261.6 38.5 %copy-start.4 = (f32[1,2,2,128]{3,2,1,0:T(2,128)S(1)}, f32[1,2,2,128]{3,2,1,0:T(2,128)}, u32[]{:S(2)}) copy-start(f32[1,2,2,128]{3,2,1,0:T(2,128)} %param.17) | copy-start | bytes 6148
  261.6 38.5 %copy-start.5 = (bf16[2,64]{1,0:T(2,128)(2,1)S(1)}, bf16[2,64]{1,0:T(2,128)(2,1)}, u32[]{:S(2)}) copy-start(bf16[2,64]{1,0:T(2,128)(2,1)} %param.16) | copy-start | bytes 772
  264.1 7.3 %collective-permute-start = (bf16[64,1,128]{2,1,0:T(2,128)(2,1)S(1)}, bf16[64,1,128]{2,1,0:T(2,128)(2,1)S(1)}, u32[]{:S(2)}, u32[]{:S(2)}) collective-permute-start(bf16[64,1,128]{2,1,0:T(2,128)(2,1)S(1)} %get-tuple-element.240), channel_id=1, source_target_pairs={{0,2},{2,4},{4,6},{6,8},{8,10},{10,12},{12,14},{14,16},{16,18},{18... | collective-permute-start | bytes 49160 | tf_op jit(solution)/shard_map/ppermute | solution.py:19
  269.4 5.2 collective-permute-start.1
  274.8 3.3 collective-permute-start.2
  276.9 5.0 collective-permute-start.3
  283.1 6.0 collective-permute-start.4
  287.2 5.2 collective-permute-start.5
  292.6 2.6 collective-permute-start.6
  293.9 5.0 collective-permute-start.7
  300.4 6.6 %collective-permute-start.8 = (bf16[64,1,128]{2,1,0:T(2,128)(2,1)S(1)}, bf16[64,1,128]{2,1,0:T(2,128)(2,1)S(1)}, u32[]{:S(2)}, u32[]{:S(2)}) collective-permute-start(bf16[64,1,128]{2,1,0:T(2,128)(2,1)S(1)} %get-tuple-element.236), channel_id=1, source_target_pairs={{0,2},{2,4},{4,6},{6,8},{8,10},{10,12},{12,14},{14,16},{16,18},{18... | collective-permute-start | bytes 49160 | tf_op jit(solution)/shard_map/ppermute | solution.py:19
  304.5 5.2 collective-permute-start.9
  309.9 5.7 collective-permute-start.10
  311.4 5.3 collective-permute-start.11
  317.9 6.1 %collective-permute-start.12 = (bf16[64,1,128]{2,1,0:T(2,128)(2,1)S(1)}, bf16[64,1,128]{2,1,0:T(2,128)(2,1)S(1)}, u32[]{:S(2)}, u32[]{:S(2)}) collective-permute-start(bf16[64,1,128]{2,1,0:T(2,128)(2,1)S(1)} %get-tuple-element.234), channel_id=1, source_target_pairs={{0,2},{2,4},{4,6},{6,8},{8,10},{10,12},{12,14},{14,16},{16,18},{18... | collective-permute-start | bytes 49160 | tf_op jit(solution)/shard_map/ppermute | solution.py:19
  321.9 5.4 collective-permute-start.13
  327.6 6.0 collective-permute-start.14
  329.6 5.3 collective-permute-start.15
Sparse Core Ops, SparseCore 0:
  9.8 53.5 all-gather.2
  67.8 114.8 all-gather.4
  337.1 260.7 all-reduce.2
where the time goes:
time: 610 us; the launch traced here: 609 us
  waiting for transfers between devices  439 us (72%)
  starting transfers between devices  45.4 us (7%)
  local copies, waits for them, and re-layouts  43.8 us (7%)
  matrix products  39.9 us (7%)
  other arithmetic  25 us (4%)
  between operations  14.5 us (2%)
    psum x1, waiting for transfers between devices, shards(): conv_grad = lax.psum(jnp.stack(conv_terms), ('dp', 'tok', 'col'))  260 us
    all_gather x1, waiting for transfers between devices, sent_together(): lax.all_gather(both, axis, axis=dim, tiled=True)  107 us
    all_gather x1, waiting for transfers between devices, shards(): all_projections = lax.all_gather(qkv_weight, 'col', axis=2, tiled=True)  50.8 us
    ppermute x8, starting transfers between devices, extended(): before = lax.ppermute(last, axis, up)  28.8 us
    dynamic_slice x32, local copies, waits for them, and re-layouts, advance(): lax.dynamic_slice_in_dim(value_rows, turn_at * block_rows, block_rows, 0)  23.8 us
    ppermute x8, waiting for transfers between devices, extended(): after = lax.ppermute(initial, axis, down)  18.7 us
    dot_general x16, matrix products, absorb(): jnp.einsum('hqk,khd->qhd', raised.astype(jnp.bfloat16), value_view, prefe...  15.2 us
    ppermute x8, starting transfers between devices, extended(): after = lax.ppermute(initial, axis, down)  12.9 us
  transfers between devices with their start and end apart: 20, of which 11 were waited for; matrix products, arithmetic and copies ran while one was open for 15% of the time, Pallas kernels for 0%

commit v1 on v0

v1 whole, which is shorter than its diff:
```python
import functools

import jax
import jax.numpy as jnp
from jax import lax
from jax.experimental import pallas as pl
from jax.experimental.pallas import tpu as pltpu
from jax.sharding import PartitionSpec as P

HEAD = 64
EPSILON = 1e-05
MESH = pl.DeviceIdType.MESH
F32 = jnp.float32
BF16 = jnp.bfloat16

NT = (((1,), (1,)), ((), ()))


def dot_nt(a, b):
    return lax.dot_general(a, b, NT, preferred_element_type=F32)


def dot_nn(a, b):
    return jnp.dot(a, b, preferred_element_type=F32)


def remote(src, dst, send_sem, recv_sem, where):
    return pltpu.make_async_remote_copy(
        src_ref=src,
        dst_ref=dst,
        send_sem=send_sem,
        recv_sem=recv_sem,
        device_id=where,
        device_id_type=MESH,
    )


QT = 256
LN_ROWS = 128


def attend_block(zs, qz, kvb, vx, m_ref, acc_ref):
    rows = kvb.shape[2]
    lane = lax.broadcasted_iota(jnp.int32, (rows, 128), 1)
    for half in range(2):
        for pair in range(2):
            v = kvb[2 * zs + half, 1, :, 128 * pair : 128 * pair + 128]
            one = jnp.ones_like(v)
            vx[2 * pair, half * rows : (half + 1) * rows, :] = jnp.where(lane < HEAD, v, one)
            vx[2 * pair + 1, half * rows : (half + 1) * rows, :] = jnp.where(lane < HEAD, one, v)

    def tile(qt, carry):
        at = pl.ds(pl.multiple_of(qt * QT, QT), QT)
        for h in range(4):
            pair = h // 2
            q = qz[h, at, :]
            s = [
                dot_nt(q, kvb[2 * zs + half, 0, :, 128 * pair : 128 * pair + 128])
                for half in range(2)
            ]
            m_old = m_ref[h, at, :]
            top = jnp.maximum(
                jnp.max(s[0], axis=1, keepdims=True), jnp.max(s[1], axis=1, keepdims=True)
            )
            m_new = jnp.maximum(m_old, top)
            wide = jnp.concatenate([m_new] * (rows // 128), axis=1)
            out = None
            for half in range(2):
                p = jnp.exp(s[half] - wide).astype(BF16)
                o = dot_nn(p, vx[h, half * rows : (half + 1) * rows, :])
                out = o if out is None else out + o
            acc_ref[h, at, :] = acc_ref[h, at, :] * jnp.exp(m_old - m_new) + out
            m_ref[h, at, :] = m_new
        return carry

    lax.fori_loop(0, qz.shape[1] // QT, tile, 0)


def attention_kernel(
    tok_ref, gain_ref, w_ref, ctx_ref, qz, kvb, vx, m_ref, acc_ref, send_sem, recv_sem
):
    t = lax.axis_index("tok")
    n_z = lax.axis_size("tok") // 2
    z, c = t // 2, lax.rem(t, 2)
    up = lax.rem(z + 1, n_z) * 2 + c
    down = lax.rem(z + n_z - 1, n_z) * 2 + c
    mate = z * 2 + 1 - c

    barrier = pltpu.get_barrier_semaphore()
    for peer in (up, down, mate):
        pl.semaphore_signal(barrier, inc=1, device_id={"tok": peer}, device_id_type=MESH)

    rows_all, width = tok_ref.shape

    def project(r, carry):
        at = pl.ds(pl.multiple_of(r * LN_ROWS, LN_ROWS), LN_ROWS)
        x = tok_ref[at, :].astype(F32)
        center = x - jnp.mean(x, axis=-1, keepdims=True)
        spread = jnp.mean(center * center, axis=-1, keepdims=True)
        normed = (center * lax.rsqrt(spread + EPSILON) * gain_ref[...].astype(F32)).astype(BF16)
        q = (dot_nn(normed, w_ref[0]).astype(BF16).astype(F32) * (1.0 / HEAD**0.5)).astype(BF16)
        kvb[t, 0, at, :] = dot_nn(normed, w_ref[1]).astype(BF16)
        kvb[t, 1, at, :] = dot_nn(normed, w_ref[2]).astype(BF16)
        lane = lax.broadcasted_iota(jnp.int32, (LN_ROWS, 128), 1)
        for pair in range(2):
            part = q[:, 128 * pair : 128 * pair + 128]
            none = jnp.zeros_like(part)
            qz[2 * pair, at, :] = jnp.where(lane < HEAD, part, none)
            qz[2 * pair + 1, at, :] = jnp.where(lane < HEAD, none, part)
        return carry

    lax.fori_loop(0, rows_all // LN_ROWS, project, 0)
    m_ref[...] = jnp.full(m_ref.shape, -1e30, F32)
    acc_ref[...] = jnp.zeros(acc_ref.shape, F32)
    pl.semaphore_wait(barrier, 3)

    def copy(blk, kv, lane_of, peer):
        piece = kvb.at[blk, kv]
        return remote(
            piece, piece, send_sem.at[lane_of, blk, kv], recv_sem.at[blk, kv], {"tok": peer}
        )

    for kv in range(2):
        copy(t, kv, 0, up).start()
        copy(t, kv, 1, down).start()
        copy(t, kv, 2, mate).start()

    def blocks(d):
        low = lax.rem(z - d + n_z, n_z)
        high = lax.rem(z + d, n_z)
        return low, high

    def turn(d, carry):
        low, high = blocks(d)

        @pl.when(jnp.logical_and(d >= 1, d <= 3))
        def _():
            for kv in range(2):
                b_low, b_high = low * 2 + c, high * 2 + c
                copy(b_low, kv, 0, up).wait_recv()

                @pl.when(d <= (3 if kv == 0 else 2))
                def _():
                    copy(b_low, kv, 0, up).start()

                copy(b_low, kv, 2, mate).start()
                copy(b_high, kv, 1, down).wait_recv()

                @pl.when(d <= (3 if kv == 1 else 2))
                def _():
                    copy(b_high, kv, 1, down).start()

                copy(b_high, kv, 2, mate).start()

        @pl.when(d == 4)
        def _():
            for kv in range(2):
                copy(low * 2 + c, kv, 0, up).wait_recv()
                copy(low * 2 + c, kv, 2, mate).start()

        for kv in range(2):
            copy(low * 2 + 1 - c, kv, 2, mate).wait_recv()

        @pl.when(jnp.logical_and(d >= 1, d <= 3))
        def _():
            for kv in range(2):
                copy(high * 2 + 1 - c, kv, 2, mate).wait_recv()

        def one(j, inner):
            attend_block(low * (1 - j) + high * j, qz, kvb, vx, m_ref, acc_ref)
            return inner

        both = jnp.where(jnp.logical_and(d >= 1, d <= 3), 2, 1)
        lax.fori_loop(0, both, one, 0)
        return carry

    lax.fori_loop(0, 5, turn, 0)

    for kv in range(2):
        copy(t, kv, 0, up).wait_send()
        copy(t, kv, 1, down).wait_send()
        copy(t, kv, 2, mate).wait_send()
        for d in range(1, 5):
            low, high = blocks(d)
            b_low, b_high = low * 2 + c, high * 2 + c
            copy(b_low, kv, 2, mate).wait_send()
            if d <= 3:
                copy(b_high, kv, 2, mate).wait_send()
            if d <= (3 if kv == 0 else 2):
                copy(b_low, kv, 0, up).wait_send()
            if d <= (3 if kv == 1 else 2):
                copy(b_high, kv, 1, down).wait_send()

    lane = lax.broadcasted_iota(jnp.int32, (rows_all, 128), 1)
    for pair in range(2):
        even, odd = acc_ref[2 * pair], acc_ref[2 * pair + 1]
        top = jnp.where(lane < HEAD, even, odd)
        total = pltpu.roll(jnp.where(lane < HEAD, odd, even), HEAD, 1)
        ctx_ref[:, 128 * pair : 128 * pair + 128] = (top / total).astype(BF16)


def attention(tokens, gain, weights):
    rows, width = tokens.shape
    n_tok = lax.axis_size("tok")
    local = weights.shape[2]
    vmem = pl.BlockSpec(memory_space=pltpu.VMEM)
    return pl.pallas_call(
        attention_kernel,
        out_shape=jax.ShapeDtypeStruct((rows, local), BF16),
        in_specs=[vmem] * 3,
        out_specs=vmem,
        scratch_shapes=[
            pltpu.VMEM((4, rows, 128), BF16),
            pltpu.VMEM((n_tok, 2, rows, local), BF16),
            pltpu.VMEM((4, 2 * rows, 128), BF16),
            pltpu.VMEM((4, rows, 128), F32),
            pltpu.VMEM((4, rows, 128), F32),
            pltpu.SemaphoreType.DMA((3, n_tok, 2)),
            pltpu.SemaphoreType.DMA((n_tok, 2)),
        ],
        compiler_params=pltpu.CompilerParams(
            collective_id=0, has_side_effects=True, vmem_limit_bytes=60 * 2**20
        ),
        name="attention",
    )(tokens, gain, weights)


RS_ROWS = 32
CG_TILES = 5
RS_CHUNKS = 14
CG_CHUNKS = 10


def pieces_of(value):
    high = value.astype(BF16)
    rest = value - high.astype(F32)
    mid = rest.astype(BF16)
    low = (rest - mid.astype(F32)).astype(BF16)
    return high, mid, low


def sigmoid(v):
    return 1.0 / (1.0 + jnp.exp(-v))


def network_kernel(
    ctx_ref,
    tok_ref,
    ow_ref,
    rwt_ref,
    cw_ref,
    cwt_ref,
    hw_ref,
    hwt_ref,
    cot_ref,
    holo_ref,
    cg_ref,
    og_ref,
    pbuf,
    ext,
    cbuf,
    st1,
    st2,
    sg,
    buf,
    rbuf,
    dbuf,
    fbuf,
    gbuf,
    p_send,
    p_recv,
    h_send,
    h_recv,
    s1,
    r1,
    s2,
    r2,
    s3,
    r3,
    s4,
    r4,
):
    t = lax.axis_index("tok")
    n_t = lax.axis_size("tok")
    dp = lax.axis_index("dp")
    n_dp = lax.axis_size("dp")
    col = lax.axis_index("col")
    other = 1 - col

    barrier = pltpu.get_barrier_semaphore()
    pl.semaphore_signal(barrier, inc=1, device_id={"col": other}, device_id_type=MESH)
    for k in range(1, n_t):
        pl.semaphore_signal(
            barrier, inc=1, device_id={"tok": lax.rem(t + k, n_t)}, device_id_type=MESH
        )
    for k in range(1, n_dp):
        pl.semaphore_signal(
            barrier, inc=1, device_id={"dp": lax.rem(dp + k, n_dp)}, device_id_type=MESH
        )

    high, mid, low = pieces_of(dot_nt(rwt_ref[...], ow_ref[...]))
    ctx = ctx_ref[...]
    pbuf[0] = dot_nt(high, ctx) + (dot_nt(mid, ctx) + dot_nt(low, ctx))
    cbuf[1, col] = cot_ref[...]
    pl.semaphore_wait(barrier, n_t + n_dp - 1)
    to_mate = {"col": other}
    c_copy = remote(cot_ref, cbuf.at[1, col], p_send.at[1], p_recv.at[1], to_mate)
    c_copy.start()
    p_copy = remote(pbuf.at[0], pbuf.at[1], p_send.at[0], p_recv.at[0], to_mate)
    p_copy.start()
    from_tokens = dot_nt(rwt_ref[...], tok_ref[...])
    p_copy.wait_recv()
    ext[2] = (from_tokens + (pbuf[0] + pbuf[1])).astype(BF16)
    c_copy.wait_recv()

    halo = []
    for k, (off, slot) in enumerate(((1, 1), (-1, 3), (2, 0), (-2, 4))):
        peer = {"tok": lax.rem(t + off + n_t, n_t)}
        halo.append(remote(ext.at[2], ext.at[slot], h_send.at[k], h_recv.at[k], peer))
        if k < 2:
            halo.append(
                remote(cbuf.at[1], cbuf.at[2 * k], h_send.at[4 + k], h_recv.at[4 + k], peer)
            )
    for item in halo:
        item.start()
    for item in halo:
        item.wait_recv()

    def in_frame(values, first_row):
        count = values.shape[1]
        row = lax.broadcasted_iota(jnp.int32, (1, count), 1) // 256 + (first_row - 4 + 2 * t)
        inside = jnp.logical_and(row >= 0, row < 2 * n_t)
        return jnp.where(inside, values, 0.0)

    def sides(values):
        count = values.shape[1]
        at = lax.broadcasted_iota(jnp.int32, (1, count), 1) % 256
        before = jnp.where(at == 0, 0.0, pltpu.roll(values, 1, 1))
        after = jnp.where(at == 255, 0.0, pltpu.roll(values, count - 1, 1))
        return before.astype(BF16), values.astype(BF16), after.astype(BF16)

    def stack(target, values, count, flip):
        shifted = sides(values)
        for a in range(3):
            for b in range(3):
                k = (3 * a + b) * 64
                row, piece = (2 - a, shifted[2 - b]) if flip else (a, shifted[b])
                target[k : k + 64, 0:count] = piece[:, row * 256 : row * 256 + count]

    x0 = in_frame(jnp.concatenate([ext[k].astype(F32) for k in range(5)], axis=1), 0)
    stack(st1, x0, 2048, False)
    pre1 = dot_nn(cw_ref[0], st1[...])
    sig1 = sigmoid(pre1)
    h1 = in_frame(pre1 * sig1, 1).astype(BF16)
    stack(st2, h1.astype(F32), 1536, False)
    pre2 = dot_nn(cw_ref[1], st2[...])
    sig2 = sigmoid(pre2)
    own2 = slice(512, 1024)
    h2 = (pre2[:, own2] * sig2[:, own2]).astype(BF16)
    holo = dot_nn(hw_ref[...], h2)
    for row in range(2):
        left = holo[:, row * 256 : row * 256 + 128]
        right = holo[:, row * 256 + 128 : row * 256 + 256]
        holo_ref[row] = jnp.where(col == 0, left, right)

    cot = jnp.concatenate(
        [cbuf[s, half, row] for s in range(3) for row in range(2) for half in range(2)], axis=1
    )
    gh2 = (hwt_ref[:, 0:1] * cot[0:1, :] + hwt_ref[:, 1:2] * cot[1:2, :]).astype(BF16)
    gp2 = in_frame(gh2.astype(F32) * sig2 * (1.0 + pre2 * (1.0 - sig2)), 2).astype(BF16)
    stack(sg, gp2.astype(F32), 1024, True)
    gh1 = dot_nn(cwt_ref[1], sg[...]).astype(BF16)
    sig1_in, pre1_in = sig1[:, 512:1536], pre1[:, 512:1536]
    gp1 = in_frame(gh1.astype(F32) * sig1_in * (1.0 + pre1_in * (1.0 - sig1_in)), 3).astype(BF16)
    stack(sg, gp1.astype(F32), 512, True)
    gh0 = dot_nn(cwt_ref[0], sg[:, 0:512]).astype(BF16)

    first = jnp.full((1, 1), col, jnp.int32) == 0
    grad = jnp.where(first, gp1[:, 256:768].astype(F32), gp2[:, own2].astype(F32)).astype(BF16)

    @pl.when(col == 0)
    def _():
        sg[:, 512:1024] = st1[:, 768:1280]

    @pl.when(col == 1)
    def _():
        sg[:, 512:1024] = st2[:, 512:1024]

    term = dot_nt(grad, sg[:, 512:1024])
    for k in range(4):
        buf[64 * k : 64 * k + 64, :] = term[:, 128 * k : 128 * k + 128]
    buf[256:320, 0:64] = term[:, 512:576]
    buf[256:320, 64:128] = jnp.zeros((64, 64), F32)
    small_term = dot_nn(gh0, ctx)
    buf[320:384, :] = small_term[:, 0:128]
    buf[384:448, :] = small_term[:, 128:256]

    def chunk(ref, i):
        return ref.at[pl.ds(pl.multiple_of(i * RS_ROWS, RS_ROWS), RS_ROWS), :]

    def phase1(k):
        peer = lax.rem(t + k, n_t)
        return peer, remote(chunk(buf, peer), rbuf.at[t], s1.at[k], r1.at[t], {"tok": peer})

    def arrival1(k):
        source = lax.rem(t + k, n_t)
        return remote(chunk(buf, 0), rbuf.at[source], s1.at[k], r1.at[source], {"tok": source})

    for k in range(1, n_t):
        peer, item = phase1(k)

        @pl.when(peer < RS_CHUNKS)
        def _():
            item.start()

    @pl.when(t < RS_CHUNKS)
    def _():
        rbuf[t] = buf[pl.ds(pl.multiple_of(t * RS_ROWS, RS_ROWS), RS_ROWS), :]
        for k in range(1, n_t):
            arrival1(k).wait_recv()
        total = rbuf[0]
        for j in range(1, n_t):
            total = total + rbuf[j]
        dbuf[dp] = total
        for k in range(1, n_dp):
            peer = lax.rem(dp + k, n_dp)
            remote(dbuf.at[dp], dbuf.at[dp], s2.at[k], r2.at[dp], {"dp": peer}).start()
        for k in range(1, n_dp):
            source = lax.rem(dp + k, n_dp)
            remote(
                dbuf.at[source], dbuf.at[source], s2.at[k], r2.at[source], {"dp": source}
            ).wait_recv()
        whole = dbuf[0]
        for j in range(1, n_dp):
            whole = whole + dbuf[j]
        fbuf[pl.ds(pl.multiple_of(t * RS_ROWS, RS_ROWS), RS_ROWS), :] = whole
        for k in range(1, n_t):
            peer = lax.rem(t + k, n_t)
            remote(chunk(fbuf, t), chunk(fbuf, t), s3.at[k], r3.at[t], {"tok": peer}).start()

    def cross(i):
        return remote(chunk(fbuf, i), chunk(gbuf, i), s4.at[i], r4.at[i], to_mate)

    for k in range(n_t):
        source = lax.rem(t + k, n_t)
        if k > 0:

            @pl.when(source < RS_CHUNKS)
            def _():
                remote(
                    chunk(fbuf, source), chunk(fbuf, source), s3.at[k], r3.at[source], {"tok": source}
                ).wait_recv()

        @pl.when(source < CG_CHUNKS)
        def _():
            cross(source).start()

    small = jnp.concatenate([fbuf[320:384, :], fbuf[384:448, :]], axis=1)
    small_t = jnp.transpose(small)
    parts = pieces_of(small_t)
    rwt = rwt_ref[...]
    og_ref[...] = dot_nn(parts[0], rwt) + (dot_nn(parts[1], rwt) + dot_nn(parts[2], rwt))

    for i in range(CG_CHUNKS):
        cross(i).wait_recv()
    for at, source in ((col, fbuf), (other, gbuf)):
        for k in range(4):
            cg_ref[at, :, 128 * k : 128 * k + 128] = source[64 * k : 64 * k + 64, :]
        cg_ref[at, :, 512:576] = source[256:320, 0:64]

    c_copy.wait_send()
    p_copy.wait_send()
    for item in halo:
        item.wait_send()
    for k in range(1, n_t):
        peer, item = phase1(k)

        @pl.when(peer < RS_CHUNKS)
        def _():
            item.wait_send()

    @pl.when(t < RS_CHUNKS)
    def _():
        for k in range(1, n_dp):
            peer = lax.rem(dp + k, n_dp)
            remote(dbuf.at[dp], dbuf.at[dp], s2.at[k], r2.at[dp], {"dp": peer}).wait_send()
        for k in range(1, n_t):
            peer = lax.rem(t + k, n_t)
            remote(chunk(fbuf, t), chunk(fbuf, t), s3.at[k], r3.at[t], {"tok": peer}).wait_send()

    for i in range(CG_CHUNKS):
        cross(i).wait_send()


def network(ctx, tokens, ow, rwt, cw, cwt, hw, hwt, cot):
    n_t, n_dp = lax.axis_size("tok"), lax.axis_size("dp")
    vmem = pl.BlockSpec(memory_space=pltpu.VMEM)
    dma = pltpu.SemaphoreType.DMA
    return pl.pallas_call(
        network_kernel,
        out_shape=(
            jax.ShapeDtypeStruct((2, 8, 128), F32),
            jax.ShapeDtypeStruct(cw.shape, F32),
            jax.ShapeDtypeStruct(ow.shape, F32),
        ),
        in_specs=[vmem] * 9,
        out_specs=(vmem,) * 3,
        scratch_shapes=[
            pltpu.VMEM((2, 64, 512), F32),
            pltpu.VMEM((5, 64, 512), BF16),
            pltpu.VMEM((3, 2, 2, 8, 128), F32),
            pltpu.VMEM((576, 2048), BF16),
            pltpu.VMEM((576, 1536), BF16),
            pltpu.VMEM((576, 1024), BF16),
            pltpu.VMEM((448, 128), F32),
            pltpu.VMEM((n_t, RS_ROWS, 128), F32),
            pltpu.VMEM((n_dp, RS_ROWS, 128), F32),
            pltpu.VMEM((448, 128), F32),
            pltpu.VMEM((320, 128), F32),
            dma((2,)),
            dma((2,)),
            dma((6,)),
            dma((6,)),
            dma((n_t,)),
            dma((n_t,)),
            dma((n_dp,)),
            dma((n_dp,)),
            dma((n_t,)),
            dma((n_t,)),
            dma((CG_CHUNKS,)),
            dma((CG_CHUNKS,)),
        ],
        compiler_params=pltpu.CompilerParams(
            collective_id=1, has_side_effects=True, vmem_limit_bytes=60 * 2**20
        ),
        name="network",
    )(ctx, tokens, ow, rwt, cw, cwt, hw, hwt, cot)


def transposed(weight):
    channels = weight.shape[0]
    return jnp.transpose(weight.reshape(channels, 9, channels), (2, 1, 0)).reshape(
        channels, 9 * channels
    )


def shards(
    tokens, ln_gain, qkv_weight, out_weight, readout_weight, conv_weight, head_weight, holo_cot
):
    rows_in = tokens[0]
    ctx = attention(rows_in, ln_gain.reshape(1, -1), qkv_weight)
    cwt = jnp.stack([transposed(conv_weight[k]) for k in range(2)])
    hw = jnp.pad(head_weight, ((0, 6), (0, 0)))
    hwt = jnp.pad(jnp.transpose(head_weight.astype(F32)), ((0, 0), (0, 126)))
    cot = jnp.pad(jnp.transpose(holo_cot[0], (1, 0, 2)), ((0, 0), (0, 6), (0, 0)))
    holo, conv_grad, out_grad = network(
        ctx, rows_in, out_weight, jnp.transpose(readout_weight), conv_weight, cwt, hw, hwt, cot
    )
    return (jnp.transpose(holo[:, 0:2], (1, 0, 2))[None], conv_grad, out_grad)


def solution(mesh):
    in_specs = (
        P("dp", "tok", None),
        P(),
        P(None, None, "col"),
        P("col", None),
        P(),
        P(),
        P(),
        P("dp", None, "tok", "col"),
    )
    out_specs = (P("dp", None, "tok", "col"), P(), P("col", None))
    return jax.shard_map(shards, mesh=mesh, in_specs=in_specs, out_specs=out_specs, check_vma=False)
```

time: 610 us -> 122 us (0.20)
  waiting for transfers between devices: 439 us -> 0 us
  Pallas kernels: 0 us -> 108 us
  starting transfers between devices: 45.4 us -> 0 us
  matrix products: 39.9 us -> 0 us
  local copies, waits for them, and re-layouts: 43.8 us -> 11.7 us
  other arithmetic: 25 us -> 1.32 us
  between operations: 14.5 us -> 0.66 us
    psum x1 -> x0, waiting for transfers between devices: 260 us -> none  [shards(): conv_grad = lax.psum(jnp.stack(conv_terms), ('dp', 'tok', 'col'))]
    all_gather x2 -> x0, waiting for transfers between devices: 158 us -> none  [the longest x1 107 us: sent_together(): lax.all_gather(both, axis, axis=dim, tiled=True)]
    pallas_call x0 -> x2, Pallas kernels: none -> 108 us  [the longest x1 63.4 us: attention(): pl.pallas_call(attention_kernel, out_shape=jax.ShapeDtypeStruct((rows, lo...]
    ppermute x16 -> x0, starting transfers between devices: 41.7 us -> none  [the longest x8 28.8 us: extended(): before = lax.ppermute(last, axis, up)]
    dot_general x46 -> x0, matrix products: 39.9 us -> none  [the longest x16 15.2 us: absorb(): jnp.einsum('hqk,khd->qhd', raised.astype(jnp.bfloat16), value_view, prefe...]
    dynamic_slice x48 -> x0, local copies, waits for them, and re-layouts: 27.2 us -> none  [the longest x32 23.8 us: advance(): lax.dynamic_slice_in_dim(value_rows, turn_at * block_rows, block_rows, 0)]
    ppermute x16 -> x0, waiting for transfers between devices: 19.7 us -> none  [the longest x8 18.7 us: extended(): after = lax.ppermute(initial, axis, down)]
    reduce_sum x18 -> x0, other arithmetic: 13.6 us -> none  [the longest x16 11.1 us: absorb(): row_total = row_total * rescale + jnp.sum(raised, axis=-1)]
  transfers between devices with their start and end apart: 20 -> 0, of which waited for: 11 -> 0; matrix products, arithmetic and copies ran while one was open for 15% -> 0% of each run, Pallas kernels for 0% -> 0%
where the time goes in v1:
time: 122 us
  Pallas kernels  108 us (89%)
  local copies, waits for them, and re-layouts  11.7 us (10%)
  other arithmetic  1.32 us (1%)
    pallas_call x1, Pallas kernels, attention(): pl.pallas_call(attention_kernel, out_shape=jax.ShapeDtypeStruct((rows, lo...  63.4 us
    pallas_call x1, Pallas kernels, network(): pl.pallas_call(network_kernel, out_shape=(jax.ShapeDtypeStruct((2, 8, 128...  44.7 us
    unnamed x7, local copies, waits for them, and re-layouts  6.34 us

profile of v1, /device:TPU:1, one launch (start us, length us, event | category | flops | bytes accessed | tf_op | source)
XLA Modules:
  0.0 121.8 jit_solution(3195552961334557957)
XLA Ops:
  0.6 0.7 copy.28
  1.3 1.2 %pad.14.hw_ref = bf16[8,64]{1,0:T(8,128)(2,1)} pad(bf16[2,64]{1,0:T(2,128)(2,1)} %param.14, bf16[]{:T(256)} %constant.4.clone.1), padding=0_6x0_0 | pad | bytes 1282 | tf_op jit(solution)/shard_map/jit(_pad)/pad | solution.py:553
  2.6 1.3 %reshape.9.gain_ref = bf16[1,1024]{1,0:T(2,128)(2,1)} reshape(bf16[1024]{0:T(1024)(128)(2,1)} %param.9) | data formatting | bytes 4096 | tf_op jit(solution)/shard_map/reshape | solution.py:551
  3.8 0.6 pad.17.cot_ref
  4.4 0.8 copy.22
  5.2 0.6 pad_convert_fusion.hwt_ref
  5.8 0.9 fusion
  6.8 0.1 copy.25
  6.9 0.2 copy.17
  7.1 0.1 copy.20
  7.2 0.1 copy.26
  7.4 0.2 copy.19
  7.5 0.1 copy.21
  7.7 0.7 pad_maximum_fusion.cwt_ref
  8.4 63.4 %attention.1.ctx_ref = bf16[512,256]{1,0:T(8,128)(2,1)} custom-call(bf16[512,1024]{1,0:T(8,128)(2,1)} %bitcast.20, bf16[1,1024]{1,0:T(2,128)(2,1)} %reshape.9.gain_ref, bf16[3,1024,256]{2,1,0:T(8,128)(2,1)} %w_ref.1), custom_call_target="tpu_custom_call" | custom-call | tf_op jit(solution)/shard_map/attention/pallas_call | solution.py:207
  71.8 44.7 %network.1 = (f32[2,8,128]{2,1,0:T(8,128)}, f32[2,64,576]{2,1,0:T(8,128)}, f32[256,1024]{1,0:T(8,128)}) custom-call(bf16[512,256]{1,0:T(8,128)(2,1)} %attention.1.ctx_ref, bf16[512,1024]{1,0:T(8,128)(2,1)} %bitcast.21, bf16[256,1024]{1,0:T(8,128)(2,1)} %ow_ref.1, bf16[64,1024]{1,0:T(8,128)(2,1)} %bitcast.26, bf16[2,64,576]{2,1,0:T(8,128)(2,1)} %cw_ref.1, ...), custom_call_target="tpu_custom_call" | custom-call | tf_op jit(solution)/shard_map/network/pallas_call | solution.py:499
  116.5 0.7 slice_bitcast_fusion
  117.2 0.6 copy.24
  117.8 1.7 %copy.31 = f32[2,64,576]{2,1,0:T(8,128)} copy(f32[2,64,576]{2,1,0:T(8,128)} %get-tuple-element.21) | data formatting | bytes 589824
  119.5 2.3 %copy.32 = f32[256,1024]{1,0:T(8,128)} copy(f32[256,1024]{1,0:T(8,128)} %get-tuple-element.22) | data formatting | bytes 2097152

commit v2 on v1

--- a/solution.py
+++ b/solution.py
@@ -35,168 +35,298 @@
     )
 
 
-QT = 256
+QT = 512
 LN_ROWS = 128
-
-
-def attend_block(zs, qz, kvb, vx, m_ref, acc_ref):
-    rows = kvb.shape[2]
-    lane = lax.broadcasted_iota(jnp.int32, (rows, 128), 1)
-    for half in range(2):
+KT = 512
+HALF = 256
+
+
+def low_lanes(shape):
+    return lax.broadcasted_iota(jnp.int32, shape, 1) < HEAD
+
+
+def swap_lanes(value):
+    return pltpu.roll(value.astype(F32), HEAD, 1)
+
+
+def attention_kernel(
+    tok_ref,
+    gain_ref,
+    w_ref,
+    ctx_ref,
+    normed_ref,
+    qout,
+    qin,
+    qz,
+    kvout,
+    kvb,
+    vx,
+    m_ref,
+    acc_ref,
+    oout,
+    oin,
+    q_send,
+    q_recv,
+    d_send,
+    m_send,
+    c_send,
+    kv_recv,
+    o_send,
+    o_recv,
+):
+    t = lax.axis_index("tok")
+    n_z = lax.axis_size("tok") // 2
+    z, c = t // 2, lax.rem(t, 2)
+    side = lax.rem(z, 2)
+    head = z // 2
+    step = 2 * side - 1
+
+    def device(chip, core):
+        return {"tok": chip * 2 + core}
+
+    def source(i):
+        return device(lax.rem(z + step * i + n_z, n_z), c)
+
+    twin = device(z + 1 - 2 * side, c)
+    mate = device(z, 1 - c)
+
+    def target(far):
+        way = step * (2 * (far % 2) - 1)
+        return lax.rem(z + way * far + 2 * n_z, n_z)
+
+    barrier = pltpu.get_barrier_semaphore()
+    for k in range(1, 4):
+        pl.semaphore_signal(barrier, inc=1, device_id=device(target(k), c), device_id_type=MESH)
+        pl.semaphore_signal(barrier, inc=1, device_id=source(k), device_id_type=MESH)
+    pl.semaphore_signal(barrier, inc=1, device_id=twin, device_id_type=MESH)
+    pl.semaphore_signal(barrier, inc=1, device_id=mate, device_id_type=MESH)
+
+    gain = gain_ref[...].astype(F32)
+    low = low_lanes((LN_ROWS, 128))
+
+    def both(r):
+        first = pl.ds(pl.multiple_of(r * LN_ROWS, LN_ROWS), LN_ROWS)
+        second = pl.ds(pl.multiple_of(HALF + r * LN_ROWS, LN_ROWS), LN_ROWS)
+        return first, second
+
+    def project_queries(r, carry):
+        first, second = both(r)
+        x = jnp.concatenate([tok_ref[first, :], tok_ref[second, :]], axis=0).astype(F32)
+        center = x - jnp.mean(x, axis=-1, keepdims=True)
+        spread = jnp.mean(center * center, axis=-1, keepdims=True)
+        normed = (center * lax.rsqrt(spread + EPSILON) * gain).astype(BF16)
+        normed_ref[first, :] = normed[0:LN_ROWS]
+        normed_ref[second, :] = normed[LN_ROWS:]
+        q = dot_nn(normed, w_ref[0])
         for pair in range(2):
-            v = kvb[2 * zs + half, 1, :, 128 * pair : 128 * pair + 128]
-            one = jnp.ones_like(v)
-            vx[2 * pair, half * rows : (half + 1) * rows, :] = jnp.where(lane < HEAD, v, one)
-            vx[2 * pair + 1, half * rows : (half + 1) * rows, :] = jnp.where(lane < HEAD, one, v)
-
-    def tile(qt, carry):
-        at = pl.ds(pl.multiple_of(qt * QT, QT), QT)
-        for h in range(4):
-            pair = h // 2
-            q = qz[h, at, :]
-            s = [
-                dot_nt(q, kvb[2 * zs + half, 0, :, 128 * pair : 128 * pair + 128])
-                for half in range(2)
-            ]
-            m_old = m_ref[h, at, :]
+            qt = q[:, 128 * pair : 128 * pair + 128]
+            q_top, q_bottom = qt[0:LN_ROWS], qt[LN_ROWS:]
+            qout[2 * pair, first, :] = jnp.where(low, q_top, swap_lanes(q_bottom)).astype(BF16)
+            qout[2 * pair + 1, first, :] = jnp.where(low, swap_lanes(q_top), q_bottom).astype(BF16)
+        return carry
+
+    def project_keys(r, carry):
+        first, second = both(r)
+        normed = jnp.concatenate([normed_ref[first, :], normed_ref[second, :]], axis=0)
+        k = dot_nn(normed, w_ref[1])
+        v = dot_nn(normed, w_ref[2])
+        for pair in range(2):
+            tile = slice(128 * pair, 128 * pair + 128)
+            kt, vt = k[:, tile], v[:, tile]
+            v_moved, k_moved = swap_lanes(vt), swap_lanes(kt)
+            for part, at in ((0, first), (1, second)):
+                rows = slice(part * LN_ROWS, (part + 1) * LN_ROWS)
+                kvout[2 * pair, at, :] = jnp.where(low, kt[rows], v_moved[rows]).astype(BF16)
+                kvout[2 * pair + 1, at, :] = jnp.where(low, k_moved[rows], vt[rows]).astype(BF16)
+        return carry
+
+    def send_q(far):
+        chip = target(far)
+        return remote(
+            qout.at[chip // 2], qin.at[far], q_send.at[far], q_recv.at[far], device(chip, c)
+        )
+
+    def send_kv(far):
+        chip = target(far)
+        return remote(
+            kvout.at[chip // 2],
+            kvb.at[2 * far, c],
+            d_send.at[far],
+            kv_recv.at[2 * far, c],
+            device(chip, c),
+        )
+
+    def own(blk):
+        return kvout.at[head] if blk == 0 else kvb.at[blk, c]
+
+    def to_twin(i):
+        there = 2 * i + 1
+        return remote(own(2 * i), kvb.at[there, c], m_send.at[i], kv_recv.at[there, c], twin)
+
+    def to_mate(blk):
+        return remote(own(blk), kvb.at[blk, c], c_send.at[blk], kv_recv.at[blk, c], mate)
+
+    def landed(blk, core):
+        piece = kvb.at[blk, core]
+        remote(piece, piece, c_send.at[blk], kv_recv.at[blk, core], mate).wait_recv()
+
+    lax.fori_loop(0, HALF // LN_ROWS, project_queries, 0)
+    pl.semaphore_wait(barrier, 8)
+    for far in range(1, 4):
+        send_q(far).start()
+    lax.fori_loop(0, HALF // LN_ROWS, project_keys, 0)
+    to_mate(0).start()
+    to_twin(0).start()
+    send_kv(1).start()
+    kvb[0, c] = kvout[head]
+    m_ref[...] = jnp.full(m_ref.shape, -1e30, F32)
+    acc_ref[...] = jnp.zeros(acc_ref.shape, F32)
+
+    low_h = low_lanes((HALF, 128))
+
+    def unpack(packed):
+        value = packed.astype(F32) * (1.0 / HEAD**0.5)
+        top = jnp.where(low_h, value, 0.0).astype(BF16)
+        bottom = jnp.where(low_h, pltpu.roll(value, HEAD, 1), 0.0).astype(BF16)
+        return top, bottom
+
+    def place(i, packed):
+        top, bottom = unpack(packed)
+        qz[i, 0:HALF, :] = top
+        qz[i, HALF : 2 * HALF, :] = bottom
+
+    place(0, qout[head])
+
+    def take(blk, i, at_v):
+        for tile in range(2 * HALF // QT):
+            at = slice(tile * QT, (tile + 1) * QT)
+            q = qz[i, at, :]
+            s = [dot_nt(q, kvb[blk, half]) for half in range(2)]
+            m_old = m_ref[i, at, :]
             top = jnp.maximum(
                 jnp.max(s[0], axis=1, keepdims=True), jnp.max(s[1], axis=1, keepdims=True)
             )
             m_new = jnp.maximum(m_old, top)
-            wide = jnp.concatenate([m_new] * (rows // 128), axis=1)
+            wide = jnp.concatenate([m_new] * (KT // 128), axis=1)
             out = None
             for half in range(2):
                 p = jnp.exp(s[half] - wide).astype(BF16)
-                o = dot_nn(p, vx[h, half * rows : (half + 1) * rows, :])
+                o = dot_nn(p, vx[at_v, half])
                 out = o if out is None else out + o
-            acc_ref[h, at, :] = acc_ref[h, at, :] * jnp.exp(m_old - m_new) + out
-            m_ref[h, at, :] = m_new
+            acc_ref[i, at, :] = acc_ref[i, at, :] * jnp.exp(m_old - m_new) + out
+            m_ref[i, at, :] = m_new
+
+    def values(blk, at_v):
+        low_k = low_lanes((KT, 128))
+        for half in range(2):
+            v = kvb[blk, half]
+            vx[at_v, half] = jnp.where(low_k, jnp.ones_like(v), v)
+
+    def send_o(i):
+        return remote(oout.at[i], oin.at[head], o_send.at[i], o_recv.at[head], source(i))
+
+    landed(0, 1 - c)
+    values(0, 0)
+
+    def first_block(i, carry):
+        @pl.when(i > 0)
+        def _():
+            remote(qin.at[i], qin.at[i], q_send.at[0], q_recv.at[i], mate).wait_recv()
+            top, bottom = unpack(qin[i])
+            qz[i, 0:HALF, :] = top
+            qz[i, HALF : 2 * HALF, :] = bottom
+
+        take(0, i, 0)
         return carry
 
-    lax.fori_loop(0, qz.shape[1] // QT, tile, 0)
-
-
-def attention_kernel(
-    tok_ref, gain_ref, w_ref, ctx_ref, qz, kvb, vx, m_ref, acc_ref, send_sem, recv_sem
-):
-    t = lax.axis_index("tok")
-    n_z = lax.axis_size("tok") // 2
-    z, c = t // 2, lax.rem(t, 2)
-    up = lax.rem(z + 1, n_z) * 2 + c
-    down = lax.rem(z + n_z - 1, n_z) * 2 + c
-    mate = z * 2 + 1 - c
-
-    barrier = pltpu.get_barrier_semaphore()
-    for peer in (up, down, mate):
-        pl.semaphore_signal(barrier, inc=1, device_id={"tok": peer}, device_id_type=MESH)
-
-    rows_all, width = tok_ref.shape
-
-    def project(r, carry):
-        at = pl.ds(pl.multiple_of(r * LN_ROWS, LN_ROWS), LN_ROWS)
-        x = tok_ref[at, :].astype(F32)
-        center = x - jnp.mean(x, axis=-1, keepdims=True)
-        spread = jnp.mean(center * center, axis=-1, keepdims=True)
-        normed = (center * lax.rsqrt(spread + EPSILON) * gain_ref[...].astype(F32)).astype(BF16)
-        q = (dot_nn(normed, w_ref[0]).astype(BF16).astype(F32) * (1.0 / HEAD**0.5)).astype(BF16)
-        kvb[t, 0, at, :] = dot_nn(normed, w_ref[1]).astype(BF16)
-        kvb[t, 1, at, :] = dot_nn(normed, w_ref[2]).astype(BF16)
-        lane = lax.broadcasted_iota(jnp.int32, (LN_ROWS, 128), 1)
-        for pair in range(2):
-            part = q[:, 128 * pair : 128 * pair + 128]
-            none = jnp.zeros_like(part)
-            qz[2 * pair, at, :] = jnp.where(lane < HEAD, part, none)
-            qz[2 * pair + 1, at, :] = jnp.where(lane < HEAD, none, part)
+    lax.fori_loop(0, 4, first_block, 0)
+
+    def relay(blk):
+        landed(blk, c)
+        remote(
+            kvb.at[blk, c],
+            kvb.at[blk + 1, c],
+            m_send.at[blk // 2],
+            kv_recv.at[blk + 1, c],
+            twin,
+        ).start()
+        pass_on(blk)
+
+    def pass_on(blk):
+        remote(kvb.at[blk, c], kvb.at[blk, c], c_send.at[blk], kv_recv.at[blk, c], mate).start()
+
+    def middle(blk, carry):
+        @pl.when(blk == 1)
+        def _():
+            send_kv(2).start()
+
+        @pl.when(blk == 2)
+        def _():
+            send_kv(3).start()
+
+        @pl.when(lax.rem(blk, 2) == 1)
+        def _():
+            landed(blk, c)
+            pass_on(blk)
+            relay(jnp.minimum(blk + 1, 6))
+
+        landed(blk, 1 - c)
+        values(blk, 0)
+
+        def each(i, inner):
+            take(blk, i, 0)
+            return inner
+
+        lax.fori_loop(0, 4, each, 0)
         return carry
 
-    lax.fori_loop(0, rows_all // LN_ROWS, project, 0)
-    m_ref[...] = jnp.full(m_ref.shape, -1e30, F32)
-    acc_ref[...] = jnp.zeros(acc_ref.shape, F32)
-    pl.semaphore_wait(barrier, 3)
-
-    def copy(blk, kv, lane_of, peer):
-        piece = kvb.at[blk, kv]
-        return remote(
-            piece, piece, send_sem.at[lane_of, blk, kv], recv_sem.at[blk, kv], {"tok": peer}
-        )
-
-    for kv in range(2):
-        copy(t, kv, 0, up).start()
-        copy(t, kv, 1, down).start()
-        copy(t, kv, 2, mate).start()
-
-    def blocks(d):
-        low = lax.rem(z - d + n_z, n_z)
-        high = lax.rem(z + d, n_z)
-        return low, high
-
-    def turn(d, carry):
-        low, high = blocks(d)
-
-        @pl.when(jnp.logical_and(d >= 1, d <= 3))
+    lax.fori_loop(1, 6, middle, 0)
+
+    landed(7, c)
+    pass_on(7)
+    for blk in (6, 7):
+        landed(blk, 1 - c)
+        values(blk, blk - 6)
+
+    def last_blocks(j, carry):
+        i = 3 - j
+
+        def each(k, inner):
+            take(6 + k, i, k)
+            return inner
+
+        lax.fori_loop(0, 2, each, 0)
+        whole = acc_ref[i]
+        done = whole / pltpu.roll(whole, HEAD, 1)
+        packed = jnp.where(low_h, pltpu.roll(done[0:HALF], HEAD, 1), done[HALF:])
+        oout[i] = packed.astype(BF16)
+
+        @pl.when(i > 0)
         def _():
-            for kv in range(2):
-                b_low, b_high = low * 2 + c, high * 2 + c
-                copy(b_low, kv, 0, up).wait_recv()
-
-                @pl.when(d <= (3 if kv == 0 else 2))
-                def _():
-                    copy(b_low, kv, 0, up).start()
-
-                copy(b_low, kv, 2, mate).start()
-                copy(b_high, kv, 1, down).wait_recv()
-
-                @pl.when(d <= (3 if kv == 1 else 2))
-                def _():
-                    copy(b_high, kv, 1, down).start()
-
-                copy(b_high, kv, 2, mate).start()
-
-        @pl.when(d == 4)
-        def _():
-            for kv in range(2):
-                copy(low * 2 + c, kv, 0, up).wait_recv()
-                copy(low * 2 + c, kv, 2, mate).start()
-
-        for kv in range(2):
-            copy(low * 2 + 1 - c, kv, 2, mate).wait_recv()
-
-        @pl.when(jnp.logical_and(d >= 1, d <= 3))
-        def _():
-            for kv in range(2):
-                copy(high * 2 + 1 - c, kv, 2, mate).wait_recv()
-
-        def one(j, inner):
-            attend_block(low * (1 - j) + high * j, qz, kvb, vx, m_ref, acc_ref)
-            return inner
-
-        both = jnp.where(jnp.logical_and(d >= 1, d <= 3), 2, 1)
-        lax.fori_loop(0, both, one, 0)
+            send_o(i).start()
+
         return carry
 
-    lax.fori_loop(0, 5, turn, 0)
-
-    for kv in range(2):
-        copy(t, kv, 0, up).wait_send()
-        copy(t, kv, 1, down).wait_send()
-        copy(t, kv, 2, mate).wait_send()
-        for d in range(1, 5):
-            low, high = blocks(d)
-            b_low, b_high = low * 2 + c, high * 2 + c
-            copy(b_low, kv, 2, mate).wait_send()
-            if d <= 3:
-                copy(b_high, kv, 2, mate).wait_send()
-            if d <= (3 if kv == 0 else 2):
-                copy(b_low, kv, 0, up).wait_send()
-            if d <= (3 if kv == 1 else 2):
-                copy(b_high, kv, 1, down).wait_send()
-
-    lane = lax.broadcasted_iota(jnp.int32, (rows_all, 128), 1)
+    lax.fori_loop(0, 4, last_blocks, 0)
+    oin[head] = oout[0]
+
+    for k in range(1, 4):
+        send_q(k).wait_send()
+        send_kv(k).wait_send()
+        send_o(k).wait_send()
+    for i in range(4):
+        to_twin(i).wait_send()
+    for blk in range(8):
+        to_mate(blk).wait_send()
+    for k in range(1, 4):
+        h = target(k) // 2
+        remote(oin.at[h], oin.at[h], o_send.at[0], o_recv.at[h], mate).wait_recv()
+
     for pair in range(2):
-        even, odd = acc_ref[2 * pair], acc_ref[2 * pair + 1]
-        top = jnp.where(lane < HEAD, even, odd)
-        total = pltpu.roll(jnp.where(lane < HEAD, odd, even), HEAD, 1)
-        ctx_ref[:, 128 * pair : 128 * pair + 128] = (top / total).astype(BF16)
+        even, odd = oin[2 * pair].astype(F32), oin[2 * pair + 1].astype(F32)
+        tile = slice(128 * pair, 128 * pair + 128)
+        ctx_ref[0:HALF, tile] = jnp.where(low_h, even, pltpu.roll(odd, HEAD, 1)).astype(BF16)
+        ctx_ref[HALF : 2 * HALF, tile] = jnp.where(low_h, pltpu.roll(even, HEAD, 1), odd).astype(BF16)
 
 
 def attention(tokens, gain, weights):
@@ -204,19 +334,32 @@
     n_tok = lax.axis_size("tok")
     local = weights.shape[2]
     vmem = pl.BlockSpec(memory_space=pltpu.VMEM)
+    dma = pltpu.SemaphoreType.DMA
     return pl.pallas_call(
         attention_kernel,
         out_shape=jax.ShapeDtypeStruct((rows, local), BF16),
         in_specs=[vmem] * 3,
         out_specs=vmem,
         scratch_shapes=[
+            pltpu.VMEM((rows, width), BF16),
+            pltpu.VMEM((4, HALF, 128), BF16),
+            pltpu.VMEM((4, HALF, 128), BF16),
             pltpu.VMEM((4, rows, 128), BF16),
-            pltpu.VMEM((n_tok, 2, rows, local), BF16),
-            pltpu.VMEM((4, 2 * rows, 128), BF16),
+            pltpu.VMEM((4, rows, 128), BF16),
+            pltpu.VMEM((8, 2, rows, 128), BF16),
+            pltpu.VMEM((2, 2, rows, 128), BF16),
             pltpu.VMEM((4, rows, 128), F32),
             pltpu.VMEM((4, rows, 128), F32),
-            pltpu.SemaphoreType.DMA((3, n_tok, 2)),
-            pltpu.SemaphoreType.DMA((n_tok, 2)),
+            pltpu.VMEM((4, HALF, 128), BF16),
+            pltpu.VMEM((4, HALF, 128), BF16),
+            dma((4,)),
+            dma((4,)),
+            dma((4,)),
+            dma((4,)),
+            dma((8,)),
+            dma((8, 2)),
+            dma((4,)),
+            dma((4,)),
         ],
         compiler_params=pltpu.CompilerParams(
             collective_id=0, has_side_effects=True, vmem_limit_bytes=60 * 2**20

time: 122 us -> 111 us (0.910)
  Pallas kernels: 108 us -> 97 us
    pallas_call x1, Pallas kernels: 63.4 us -> 52.8 us  [attention(): pl.pallas_call(attention_kernel, out_shape=jax.ShapeDtypeStruct((rows, lo...]
where the time goes in v2:
time: 111 us
  Pallas kernels  97 us (87%)
  local copies, waits for them, and re-layouts  11.7 us (11%)
  other arithmetic  1.32 us (1%)
    pallas_call x1, Pallas kernels, attention(): pl.pallas_call(attention_kernel, out_shape=jax.ShapeDtypeStruct((rows, lo...  52.8 us
    pallas_call x1, Pallas kernels, network(): pl.pallas_call(network_kernel, out_shape=(jax.ShapeDtypeStruct((2, 8, 128...  44.1 us
    unnamed x7, local copies, waits for them, and re-layouts  6.34 us

profile of v2, /device:TPU:1, one launch (start us, length us, event | category | flops | bytes accessed | tf_op | source)
XLA Modules:
  0.0 110.7 jit_solution(10744498052897680895)
XLA Ops:
  0.6 0.7 copy.28
  1.3 1.2 %pad.14.hw_ref = bf16[8,64]{1,0:T(8,128)(2,1)} pad(bf16[2,64]{1,0:T(2,128)(2,1)} %param.14, bf16[]{:T(256)} %constant.4.clone.1), padding=0_6x0_0 | pad | bytes 1282 | tf_op jit(solution)/shard_map/jit(_pad)/pad | solution.py:696
  2.6 1.3 %reshape.9.gain_ref = bf16[1,1024]{1,0:T(2,128)(2,1)} reshape(bf16[1024]{0:T(1024)(128)(2,1)} %param.9) | data formatting | bytes 4096 | tf_op jit(solution)/shard_map/reshape | solution.py:694
  3.8 0.6 pad.17.cot_ref
  4.4 0.8 copy.22
  5.2 0.6 pad_convert_fusion.hwt_ref
  5.8 0.9 fusion
  6.8 0.1 copy.25
  6.9 0.2 copy.17
  7.1 0.1 copy.20
  7.2 0.1 copy.26
  7.4 0.2 copy.19
  7.5 0.1 copy.21
  7.7 0.7 pad_maximum_fusion.cwt_ref
  8.4 52.8 %attention.1.ctx_ref = bf16[512,256]{1,0:T(8,128)(2,1)} custom-call(bf16[512,1024]{1,0:T(8,128)(2,1)} %bitcast.20, bf16[1,1024]{1,0:T(2,128)(2,1)} %reshape.9.gain_ref, bf16[3,1024,256]{2,1,0:T(8,128)(2,1)} %w_ref.1), custom_call_target="tpu_custom_call" | custom-call | tf_op jit(solution)/shard_map/attention/pallas_call | solution.py:338
  61.2 44.1 %network.1 = (f32[2,8,128]{2,1,0:T(8,128)}, f32[2,64,576]{2,1,0:T(8,128)}, f32[256,1024]{1,0:T(8,128)}) custom-call(bf16[512,256]{1,0:T(8,128)(2,1)} %attention.1.ctx_ref, bf16[512,1024]{1,0:T(8,128)(2,1)} %bitcast.21, bf16[256,1024]{1,0:T(8,128)(2,1)} %ow_ref.1, bf16[64,1024]{1,0:T(8,128)(2,1)} %bitcast.26, bf16[2,64,576]{2,1,0:T(8,128)(2,1)} %cw_ref.1, ...), custom_call_target="tpu_custom_call" | custom-call | tf_op jit(solution)/shard_map/network/pallas_call | solution.py:642
  105.3 0.7 slice_bitcast_fusion
  106.0 0.6 copy.24
  106.6 1.7 %copy.31 = f32[2,64,576]{2,1,0:T(8,128)} copy(f32[2,64,576]{2,1,0:T(8,128)} %get-tuple-element.21) | data formatting | bytes 589824
  108.3 2.3 %copy.32 = f32[256,1024]{1,0:T(8,128)} copy(f32[256,1024]{1,0:T(8,128)} %get-tuple-element.22) | data formatting | bytes 2097152

commit v3 on v2

--- a/solution.py
+++ b/solution.py
@@ -101,7 +101,7 @@
     pl.semaphore_signal(barrier, inc=1, device_id=twin, device_id_type=MESH)
     pl.semaphore_signal(barrier, inc=1, device_id=mate, device_id_type=MESH)
 
-    gain = gain_ref[...].astype(F32)
+    gain = gain_ref[...].astype(F32).reshape(1, -1)
     low = low_lanes((LN_ROWS, 128))
 
     def both(r):
@@ -392,13 +392,12 @@
     ow_ref,
     rwt_ref,
     cw_ref,
-    cwt_ref,
     hw_ref,
-    hwt_ref,
     cot_ref,
     holo_ref,
-    cg_ref,
-    og_ref,
+    own_ref,
+    other_ref,
+    cwt_ref,
     pbuf,
     ext,
     cbuf,
@@ -448,10 +447,15 @@
     pl.semaphore_wait(barrier, n_t + n_dp - 1)
     to_mate = {"col": other}
     c_copy = remote(cot_ref, cbuf.at[1, col], p_send.at[1], p_recv.at[1], to_mate)
-    c_copy.start()
     p_copy = remote(pbuf.at[0], pbuf.at[1], p_send.at[0], p_recv.at[0], to_mate)
     p_copy.start()
+    c_copy.start()
     from_tokens = dot_nt(rwt_ref[...], tok_ref[...])
+    for layer in range(2):
+        for k in range(9):
+            tap = slice(64 * k, 64 * k + 64)
+            turned = jnp.transpose(cw_ref[layer, :, tap].astype(F32))
+            cwt_ref[layer, :, tap] = turned.astype(BF16)
     p_copy.wait_recv()
     ext[2] = (from_tokens + (pbuf[0] + pbuf[1])).astype(BF16)
     c_copy.wait_recv()
@@ -504,12 +508,26 @@
     for row in range(2):
         left = holo[:, row * 256 : row * 256 + 128]
         right = holo[:, row * 256 + 128 : row * 256 + 256]
-        holo_ref[row] = jnp.where(col == 0, left, right)
-
-    cot = jnp.concatenate(
-        [cbuf[s, half, row] for s in range(3) for row in range(2) for half in range(2)], axis=1
+        holo_ref[:, row, :] = jnp.where(col == 0, left, right)
+
+    diagonal = lax.broadcasted_iota(jnp.int32, (64, 64), 0) == lax.broadcasted_iota(
+        jnp.int32, (64, 64), 1
     )
-    gh2 = (hwt_ref[:, 0:1] * cot[0:1, :] + hwt_ref[:, 1:2] * cot[1:2, :]).astype(BF16)
+    raised = None
+    for k in range(2):
+        cot = jnp.concatenate(
+            [
+                cbuf[s, half, k, row : row + 1, :]
+                for s in range(3)
+                for row in range(2)
+                for half in range(2)
+            ],
+            axis=1,
+        )
+        weight = jnp.where(diagonal, hw_ref[k : k + 1, :].astype(F32), 0.0)
+        product = jnp.sum(weight, axis=1, keepdims=True) * cot
+        raised = product if raised is None else raised + product
+    gh2 = raised.astype(BF16)
     gp2 = in_frame(gh2.astype(F32) * sig2 * (1.0 + pre2 * (1.0 - sig2)), 2).astype(BF16)
     stack(sg, gp2.astype(F32), 1024, True)
     gh1 = dot_nn(cwt_ref[1], sg[...]).astype(BF16)
@@ -576,7 +594,7 @@
         whole = dbuf[0]
         for j in range(1, n_dp):
             whole = whole + dbuf[j]
-        fbuf[pl.ds(pl.multiple_of(t * RS_ROWS, RS_ROWS), RS_ROWS), :] = whole
+        fbuf[pl.ds(pl.multiple_of(t * RS_ROWS, RS_ROWS), RS_ROWS), :] = whole.astype(BF16)
         for k in range(1, n_t):
             peer = lax.rem(t + k, n_t)
             remote(chunk(fbuf, t), chunk(fbuf, t), s3.at[k], r3.at[t], {"tok": peer}).start()
@@ -584,7 +602,7 @@
     def cross(i):
         return remote(chunk(fbuf, i), chunk(gbuf, i), s4.at[i], r4.at[i], to_mate)
 
-    for k in range(n_t):
+    for k in sorted(range(n_t), key=lambda k: min(k, n_t - k)):
         source = lax.rem(t + k, n_t)
         if k > 0:
 
@@ -598,18 +616,10 @@
         def _():
             cross(source).start()
 
-    small = jnp.concatenate([fbuf[320:384, :], fbuf[384:448, :]], axis=1)
-    small_t = jnp.transpose(small)
-    parts = pieces_of(small_t)
-    rwt = rwt_ref[...]
-    og_ref[...] = dot_nn(parts[0], rwt) + (dot_nn(parts[1], rwt) + dot_nn(parts[2], rwt))
-
+    own_ref[...] = fbuf[...]
     for i in range(CG_CHUNKS):
         cross(i).wait_recv()
-    for at, source in ((col, fbuf), (other, gbuf)):
-        for k in range(4):
-            cg_ref[at, :, 128 * k : 128 * k + 128] = source[64 * k : 64 * k + 64, :]
-        cg_ref[at, :, 512:576] = source[256:320, 0:64]
+    other_ref[...] = gbuf[...]
 
     c_copy.wait_send()
     p_copy.wait_send()
@@ -635,31 +645,32 @@
         cross(i).wait_send()
 
 
-def network(ctx, tokens, ow, rwt, cw, cwt, hw, hwt, cot):
+def network(ctx, tokens, ow, rwt, cw, hw, cot):
     n_t, n_dp = lax.axis_size("tok"), lax.axis_size("dp")
     vmem = pl.BlockSpec(memory_space=pltpu.VMEM)
     dma = pltpu.SemaphoreType.DMA
     return pl.pallas_call(
         network_kernel,
         out_shape=(
-            jax.ShapeDtypeStruct((2, 8, 128), F32),
-            jax.ShapeDtypeStruct(cw.shape, F32),
-            jax.ShapeDtypeStruct(ow.shape, F32),
+            jax.ShapeDtypeStruct(cot.shape, F32),
+            jax.ShapeDtypeStruct((448, 128), BF16),
+            jax.ShapeDtypeStruct((320, 128), BF16),
         ),
-        in_specs=[vmem] * 9,
+        in_specs=[vmem] * 7,
         out_specs=(vmem,) * 3,
         scratch_shapes=[
+            pltpu.VMEM((2, 64, 576), BF16),
             pltpu.VMEM((2, 64, 512), F32),
             pltpu.VMEM((5, 64, 512), BF16),
-            pltpu.VMEM((3, 2, 2, 8, 128), F32),
+            pltpu.VMEM((3, 2, 2, 2, 128), F32),
             pltpu.VMEM((576, 2048), BF16),
             pltpu.VMEM((576, 1536), BF16),
             pltpu.VMEM((576, 1024), BF16),
             pltpu.VMEM((448, 128), F32),
             pltpu.VMEM((n_t, RS_ROWS, 128), F32),
             pltpu.VMEM((n_dp, RS_ROWS, 128), F32),
-            pltpu.VMEM((448, 128), F32),
-            pltpu.VMEM((320, 128), F32),
+            pltpu.VMEM((448, 128), BF16),
+            pltpu.VMEM((320, 128), BF16),
             dma((2,)),
             dma((2,)),
             dma((6,)),
@@ -677,29 +688,45 @@
             collective_id=1, has_side_effects=True, vmem_limit_bytes=60 * 2**20
         ),
         name="network",
-    )(ctx, tokens, ow, rwt, cw, cwt, hw, hwt, cot)
-
-
-def transposed(weight):
-    channels = weight.shape[0]
-    return jnp.transpose(weight.reshape(channels, 9, channels), (2, 1, 0)).reshape(
-        channels, 9 * channels
-    )
+    )(ctx, tokens, ow, rwt, cw, hw, cot)
+
+
+def finish_kernel(holo_in, own_ref, other_ref, rwt_ref, holo_ref, cg_ref, og_ref):
+    col = lax.axis_index("col")
+    small = jnp.concatenate([own_ref[320:384, :], own_ref[384:448, :]], axis=1)
+    og_ref[...] = dot_nn(jnp.transpose(small.astype(F32)).astype(BF16), rwt_ref[...])
+    for at, source in ((col, own_ref), (1 - col, other_ref)):
+        for k in range(4):
+            cg_ref[at, :, 128 * k : 128 * k + 128] = source[64 * k : 64 * k + 64, :].astype(F32)
+        cg_ref[at, :, 512:576] = source[256:320, 0:64].astype(F32)
+    holo_ref[0] = holo_in[...]
+
+
+def finish(holo, own, other, rwt, cw, ow):
+    vmem = pl.BlockSpec(memory_space=pltpu.VMEM)
+    return pl.pallas_call(
+        finish_kernel,
+        out_shape=(
+            jax.ShapeDtypeStruct((1, *holo.shape), F32),
+            jax.ShapeDtypeStruct(cw.shape, F32),
+            jax.ShapeDtypeStruct(ow.shape, F32),
+        ),
+        in_specs=[vmem] * 4,
+        out_specs=(vmem,) * 3,
+        name="finish",
+    )(holo, own, other, rwt)
 
 
 def shards(
     tokens, ln_gain, qkv_weight, out_weight, readout_weight, conv_weight, head_weight, holo_cot
 ):
     rows_in = tokens[0]
-    ctx = attention(rows_in, ln_gain.reshape(1, -1), qkv_weight)
-    cwt = jnp.stack([transposed(conv_weight[k]) for k in range(2)])
-    hw = jnp.pad(head_weight, ((0, 6), (0, 0)))
-    hwt = jnp.pad(jnp.transpose(head_weight.astype(F32)), ((0, 0), (0, 126)))
-    cot = jnp.pad(jnp.transpose(holo_cot[0], (1, 0, 2)), ((0, 0), (0, 6), (0, 0)))
-    holo, conv_grad, out_grad = network(
-        ctx, rows_in, out_weight, jnp.transpose(readout_weight), conv_weight, cwt, hw, hwt, cot
+    ctx = attention(rows_in, ln_gain, qkv_weight)
+    rwt = jnp.transpose(readout_weight)
+    holo, own, other = network(
+        ctx, rows_in, out_weight, rwt, conv_weight, head_weight, holo_cot[0]
     )
-    return (jnp.transpose(holo[:, 0:2], (1, 0, 2))[None], conv_grad, out_grad)
+    return finish(holo, own, other, rwt, conv_weight, out_weight)
 
 
 def solution(mesh):

time: 111 us -> 96.6 us (0.87)
  local copies, waits for them, and re-layouts: 11.7 us -> 0 us
  other arithmetic: 1.32 us -> 0 us
  Pallas kernels: 97 us -> 95.8 us
    unnamed x7 -> x0, local copies, waits for them, and re-layouts: 6.34 us -> none
    pad x2 -> x0, local copies, waits for them, and re-layouts: 1.84 us -> none  [the longest x1 1.24 us: shards(): hw = jnp.pad(head_weight, ((0, 6), (0, 0)))]
    pallas_call x1 -> x2, Pallas kernels: 44.1 us -> 42.8 us  [the longest x1 40.5 us: network(): pl.pallas_call(network_kernel, out_shape=(jax.ShapeDtypeStruct(cot.shape,...]
    reshape x1 -> x0, local copies, waits for them, and re-layouts: 1.27 us -> none  [shards(): ctx = attention(rows_in, ln_gain.reshape(1, -1), qkv_weight)]
where the time goes in v3:
time: 96.6 us; the launch traced here: 96.5 us
  Pallas kernels  95.8 us (99%)
    pallas_call x1, Pallas kernels, attention(): pl.pallas_call(attention_kernel, out_shape=jax.ShapeDtypeStruct((rows, lo...  53 us
    pallas_call x1, Pallas kernels, network(): pl.pallas_call(network_kernel, out_shape=(jax.ShapeDtypeStruct(cot.shape,...  40.5 us
    pallas_call x1, Pallas kernels, finish(): pl.pallas_call(finish_kernel, out_shape=(jax.ShapeDtypeStruct((1, *holo.s...  2.36 us

profile of v3, /device:TPU:1, one launch (start us, length us, event | category | flops | bytes accessed | tf_op | source)
XLA Modules:
  0.0 96.5 jit_solution(4055001395708805395)
XLA Ops:
  0.6 53.0 %attention.1.ctx_ref = bf16[512,256]{1,0:T(8,128)(2,1)} custom-call(bf16[512,1024]{1,0:T(8,128)(2,1)} %bitcast.3, bf16[1024]{0:T(1024)(128)(2,1)} %gain_ref.1, bf16[3,1024,256]{2,1,0:T(8,128)(2,1)} %w_ref.1), custom_call_target="tpu_custom_call" | custom-call | tf_op jit(solution)/shard_map/attention/pallas_call | solution.py:338
  53.6 40.5 %network.1 = (f32[2,2,128]{2,1,0:T(2,128)}, bf16[448,128]{1,0:T(8,128)(2,1)}, bf16[320,128]{1,0:T(8,128)(2,1)}) custom-call(bf16[512,256]{1,0:T(8,128)(2,1)} %attention.1.ctx_ref, bf16[512,1024]{1,0:T(8,128)(2,1)} %bitcast.4, bf16[256,1024]{1,0:T(8,128)(2,1)} %ow_ref.1, bf16[64,1024]{1,0:T(8,128)(2,1)} %bitcast.5, bf16[2,64,576]{2,1,0:T(8,128)(2,1)} %cw_ref.1, ...), custom_call_target="tpu_custom_call" | custom-call | tf_op jit(solution)/shard_map/network/pallas_call | solution.py:652
  94.1 2.4 %finish.1 = (f32[1,2,2,128]{3,2,1,0:T(2,128)}, f32[2,64,576]{2,1,0:T(8,128)}, f32[256,1024]{1,0:T(8,128)}) custom-call(f32[2,2,128]{2,1,0:T(2,128)} %get-tuple-element.6.holo_in, bf16[448,128]{1,0:T(8,128)(2,1)} %get-tuple-element.7.own_ref, bf16[320,128]{1,0:T(8,128)(2,1)} %get-tuple-element.8.other_ref, bf16[64,1024]{1,0:T(8,128)(2,1)} %bitcast.6), custom_call_target="tpu_custom_call" | custom-call | tf_op jit(solution)/shard_map/finish/pallas_call | solution.py:707

commit v4 on v3

--- a/solution.py
+++ b/solution.py
@@ -49,7 +49,9 @@
     return pltpu.roll(value.astype(F32), HEAD, 1)
 
 
-def attention_kernel(
+def attention_part(
+    ready,
+    meanwhile,
     tok_ref,
     gain_ref,
     w_ref,
@@ -94,13 +96,6 @@
         way = step * (2 * (far % 2) - 1)
         return lax.rem(z + way * far + 2 * n_z, n_z)
 
-    barrier = pltpu.get_barrier_semaphore()
-    for k in range(1, 4):
-        pl.semaphore_signal(barrier, inc=1, device_id=device(target(k), c), device_id_type=MESH)
-        pl.semaphore_signal(barrier, inc=1, device_id=source(k), device_id_type=MESH)
-    pl.semaphore_signal(barrier, inc=1, device_id=twin, device_id_type=MESH)
-    pl.semaphore_signal(barrier, inc=1, device_id=mate, device_id_type=MESH)
-
     gain = gain_ref[...].astype(F32).reshape(1, -1)
     low = low_lanes((LN_ROWS, 128))
 
@@ -171,7 +166,7 @@
         remote(piece, piece, c_send.at[blk], kv_recv.at[blk, core], mate).wait_recv()
 
     lax.fori_loop(0, HALF // LN_ROWS, project_queries, 0)
-    pl.semaphore_wait(barrier, 8)
+    ready()
     for far in range(1, 4):
         send_q(far).start()
     lax.fori_loop(0, HALF // LN_ROWS, project_keys, 0)
@@ -179,6 +174,7 @@
     to_twin(0).start()
     send_kv(1).start()
     kvb[0, c] = kvout[head]
+    meanwhile()
     m_ref[...] = jnp.full(m_ref.shape, -1e30, F32)
     acc_ref[...] = jnp.zeros(acc_ref.shape, F32)
 
@@ -329,45 +325,6 @@
         ctx_ref[HALF : 2 * HALF, tile] = jnp.where(low_h, pltpu.roll(even, HEAD, 1), odd).astype(BF16)
 
 
-def attention(tokens, gain, weights):
-    rows, width = tokens.shape
-    n_tok = lax.axis_size("tok")
-    local = weights.shape[2]
-    vmem = pl.BlockSpec(memory_space=pltpu.VMEM)
-    dma = pltpu.SemaphoreType.DMA
-    return pl.pallas_call(
-        attention_kernel,
-        out_shape=jax.ShapeDtypeStruct((rows, local), BF16),
-        in_specs=[vmem] * 3,
-        out_specs=vmem,
-        scratch_shapes=[
-            pltpu.VMEM((rows, width), BF16),
-            pltpu.VMEM((4, HALF, 128), BF16),
-            pltpu.VMEM((4, HALF, 128), BF16),
-            pltpu.VMEM((4, rows, 128), BF16),
-            pltpu.VMEM((4, rows, 128), BF16),
-            pltpu.VMEM((8, 2, rows, 128), BF16),
-            pltpu.VMEM((2, 2, rows, 128), BF16),
-            pltpu.VMEM((4, rows, 128), F32),
-            pltpu.VMEM((4, rows, 128), F32),
-            pltpu.VMEM((4, HALF, 128), BF16),
-            pltpu.VMEM((4, HALF, 128), BF16),
-            dma((4,)),
-            dma((4,)),
-            dma((4,)),
-            dma((4,)),
-            dma((8,)),
-            dma((8, 2)),
-            dma((4,)),
-            dma((4,)),
-        ],
-        compiler_params=pltpu.CompilerParams(
-            collective_id=0, has_side_effects=True, vmem_limit_bytes=60 * 2**20
-        ),
-        name="attention",
-    )(tokens, gain, weights)
-
-
 RS_ROWS = 32
 CG_TILES = 5
 RS_CHUNKS = 14
@@ -386,9 +343,10 @@
     return 1.0 / (1.0 + jnp.exp(-v))
 
 
-def network_kernel(
-    ctx_ref,
+def step_kernel(
     tok_ref,
+    gain_ref,
+    w_ref,
     ow_ref,
     rwt_ref,
     cw_ref,
@@ -397,6 +355,9 @@
     holo_ref,
     own_ref,
     other_ref,
+    ctx_ref,
+    w2_ref,
+    base_ref,
     cwt_ref,
     pbuf,
     ext,
@@ -421,6 +382,7 @@
     r3,
     s4,
     r4,
+    *attention_refs,
 ):
     t = lax.axis_index("tok")
     n_t = lax.axis_size("tok")
@@ -440,24 +402,32 @@
             barrier, inc=1, device_id={"dp": lax.rem(dp + k, n_dp)}, device_id_type=MESH
         )
 
-    high, mid, low = pieces_of(dot_nt(rwt_ref[...], ow_ref[...]))
-    ctx = ctx_ref[...]
-    pbuf[0] = dot_nt(high, ctx) + (dot_nt(mid, ctx) + dot_nt(low, ctx))
-    cbuf[1, col] = cot_ref[...]
-    pl.semaphore_wait(barrier, n_t + n_dp - 1)
     to_mate = {"col": other}
     c_copy = remote(cot_ref, cbuf.at[1, col], p_send.at[1], p_recv.at[1], to_mate)
+
+    def ready():
+        pl.semaphore_wait(barrier, n_t + n_dp - 1)
+
+    def meanwhile():
+        c_copy.start()
+        cbuf[1, col] = cot_ref[...]
+        for k, piece in enumerate(pieces_of(dot_nt(rwt_ref[...], ow_ref[...]))):
+            w2_ref[k] = piece
+        base_ref[...] = dot_nt(rwt_ref[...], tok_ref[...])
+        for layer in range(2):
+            for k in range(9):
+                tap = slice(64 * k, 64 * k + 64)
+                turned = jnp.transpose(cw_ref[layer, :, tap].astype(F32))
+                cwt_ref[layer, :, tap] = turned.astype(BF16)
+
+    attention_part(ready, meanwhile, tok_ref, gain_ref, w_ref, ctx_ref, *attention_refs)
+
+    ctx = ctx_ref[...]
+    pbuf[0] = dot_nt(w2_ref[0], ctx) + (dot_nt(w2_ref[1], ctx) + dot_nt(w2_ref[2], ctx))
     p_copy = remote(pbuf.at[0], pbuf.at[1], p_send.at[0], p_recv.at[0], to_mate)
     p_copy.start()
-    c_copy.start()
-    from_tokens = dot_nt(rwt_ref[...], tok_ref[...])
-    for layer in range(2):
-        for k in range(9):
-            tap = slice(64 * k, 64 * k + 64)
-            turned = jnp.transpose(cw_ref[layer, :, tap].astype(F32))
-            cwt_ref[layer, :, tap] = turned.astype(BF16)
     p_copy.wait_recv()
-    ext[2] = (from_tokens + (pbuf[0] + pbuf[1])).astype(BF16)
+    ext[2] = (base_ref[...] + (pbuf[0] + pbuf[1])).astype(BF16)
     c_copy.wait_recv()
 
     halo = []
@@ -549,12 +519,12 @@
 
     term = dot_nt(grad, sg[:, 512:1024])
     for k in range(4):
-        buf[64 * k : 64 * k + 64, :] = term[:, 128 * k : 128 * k + 128]
-    buf[256:320, 0:64] = term[:, 512:576]
-    buf[256:320, 64:128] = jnp.zeros((64, 64), F32)
+        buf[64 * k : 64 * k + 64, :] = term[:, 128 * k : 128 * k + 128].astype(BF16)
+    buf[256:320, 0:64] = term[:, 512:576].astype(BF16)
+    buf[256:320, 64:128] = jnp.zeros((64, 64), BF16)
     small_term = dot_nn(gh0, ctx)
-    buf[320:384, :] = small_term[:, 0:128]
-    buf[384:448, :] = small_term[:, 128:256]
+    buf[320:384, :] = small_term[:, 0:128].astype(BF16)
+    buf[384:448, :] = small_term[:, 128:256].astype(BF16)
 
     def chunk(ref, i):
         return ref.at[pl.ds(pl.multiple_of(i * RS_ROWS, RS_ROWS), RS_ROWS), :]
@@ -579,9 +549,9 @@
         rbuf[t] = buf[pl.ds(pl.multiple_of(t * RS_ROWS, RS_ROWS), RS_ROWS), :]
         for k in range(1, n_t):
             arrival1(k).wait_recv()
-        total = rbuf[0]
+        total = rbuf[0].astype(F32)
         for j in range(1, n_t):
-            total = total + rbuf[j]
+            total = total + rbuf[j].astype(F32)
         dbuf[dp] = total
         for k in range(1, n_dp):
             peer = lax.rem(dp + k, n_dp)
@@ -645,20 +615,26 @@
         cross(i).wait_send()
 
 
-def network(ctx, tokens, ow, rwt, cw, hw, cot):
+def step(tokens, gain, weights, ow, rwt, cw, hw, cot):
+    rows, width = tokens.shape
+    n_tok = lax.axis_size("tok")
+    local = weights.shape[2]
     n_t, n_dp = lax.axis_size("tok"), lax.axis_size("dp")
     vmem = pl.BlockSpec(memory_space=pltpu.VMEM)
     dma = pltpu.SemaphoreType.DMA
     return pl.pallas_call(
-        network_kernel,
+        step_kernel,
         out_shape=(
             jax.ShapeDtypeStruct(cot.shape, F32),
             jax.ShapeDtypeStruct((448, 128), BF16),
             jax.ShapeDtypeStruct((320, 128), BF16),
         ),
-        in_specs=[vmem] * 7,
+        in_specs=[vmem] * 8,
         out_specs=(vmem,) * 3,
         scratch_shapes=[
+            pltpu.VMEM((rows, local), BF16),
+            pltpu.VMEM((3, 64, local), BF16),
+            pltpu.VMEM((64, rows), F32),
             pltpu.VMEM((2, 64, 576), BF16),
             pltpu.VMEM((2, 64, 512), F32),
             pltpu.VMEM((5, 64, 512), BF16),
@@ -666,8 +642,8 @@
             pltpu.VMEM((576, 2048), BF16),
             pltpu.VMEM((576, 1536), BF16),
             pltpu.VMEM((576, 1024), BF16),
-            pltpu.VMEM((448, 128), F32),
-            pltpu.VMEM((n_t, RS_ROWS, 128), F32),
+            pltpu.VMEM((448, 128), BF16),
+            pltpu.VMEM((n_t, RS_ROWS, 128), BF16),
             pltpu.VMEM((n_dp, RS_ROWS, 128), F32),
             pltpu.VMEM((448, 128), BF16),
             pltpu.VMEM((320, 128), BF16),
@@ -683,12 +659,31 @@
             dma((n_t,)),
             dma((CG_CHUNKS,)),
             dma((CG_CHUNKS,)),
+            pltpu.VMEM((rows, width), BF16),
+            pltpu.VMEM((4, HALF, 128), BF16),
+            pltpu.VMEM((4, HALF, 128), BF16),
+            pltpu.VMEM((4, rows, 128), BF16),
+            pltpu.VMEM((4, rows, 128), BF16),
+            pltpu.VMEM((8, 2, rows, 128), BF16),
+            pltpu.VMEM((2, 2, rows, 128), BF16),
+            pltpu.VMEM((4, rows, 128), F32),
+            pltpu.VMEM((4, rows, 128), F32),
+            pltpu.VMEM((4, HALF, 128), BF16),
+            pltpu.VMEM((4, HALF, 128), BF16),
+            dma((4,)),
+            dma((4,)),
+            dma((4,)),
+            dma((4,)),
+            dma((8,)),
+            dma((8, 2)),
+            dma((4,)),
+            dma((4,)),
         ],
         compiler_params=pltpu.CompilerParams(
-            collective_id=1, has_side_effects=True, vmem_limit_bytes=60 * 2**20
+            collective_id=0, has_side_effects=True, vmem_limit_bytes=60 * 2**20
         ),
-        name="network",
-    )(ctx, tokens, ow, rwt, cw, hw, cot)
+        name="step",
+    )(tokens, gain, weights, ow, rwt, cw, hw, cot)
 
 
 def finish_kernel(holo_in, own_ref, other_ref, rwt_ref, holo_ref, cg_ref, og_ref):
@@ -721,10 +716,9 @@
     tokens, ln_gain, qkv_weight, out_weight, readout_weight, conv_weight, head_weight, holo_cot
 ):
     rows_in = tokens[0]
-    ctx = attention(rows_in, ln_gain, qkv_weight)
     rwt = jnp.transpose(readout_weight)
-    holo, own, other = network(
-        ctx, rows_in, out_weight, rwt, conv_weight, head_weight, holo_cot[0]
+    holo, own, other = step(
+        rows_in, ln_gain, qkv_weight, out_weight, rwt, conv_weight, head_weight, holo_cot[0]
     )
     return finish(holo, own, other, rwt, conv_weight, out_weight)
 

time: 96.6 us -> 90.5 us (0.937)
  Pallas kernels: 95.8 us -> 89.7 us
    pallas_call x2 -> x1, Pallas kernels: 93.4 us -> 87.4 us  [step(): pl.pallas_call(step_kernel, out_shape=(jax.ShapeDtypeStruct(cot.shape, F3...]
where the time goes in v4:
time: 90.5 us; the launch traced here: 90.4 us
  Pallas kernels  89.7 us (99%)
    pallas_call x1, Pallas kernels, step(): pl.pallas_call(step_kernel, out_shape=(jax.ShapeDtypeStruct(cot.shape, F3...  87.4 us
    pallas_call x1, Pallas kernels, finish(): pl.pallas_call(finish_kernel, out_shape=(jax.ShapeDtypeStruct((1, *holo.s...  2.37 us

profile of v4, /device:TPU:1, one launch (start us, length us, event | category | flops | bytes accessed | tf_op | source)
XLA Modules:
  0.0 90.4 jit_solution(11697842742197112406)
XLA Ops:
  0.6 87.4 %step.1 = (f32[2,2,128]{2,1,0:T(2,128)}, bf16[448,128]{1,0:T(8,128)(2,1)}, bf16[320,128]{1,0:T(8,128)(2,1)}) custom-call(bf16[512,1024]{1,0:T(8,128)(2,1)} %bitcast.3, bf16[1024]{0:T(1024)(128)(2,1)} %gain_ref.1, bf16[3,1024,256]{2,1,0:T(8,128)(2,1)} %w_ref.1, bf16[256,1024]{1,0:T(8,128)(2,1)} %ow_ref.1, bf16[64,1024]{1,0:T(8,128)(2,1)} %bitcast.4, ...), custom_call_target="tpu_custom_call" | custom-call | tf_op jit(solution)/shard_map/step/pallas_call | solution.py:625
  88.0 2.4 %finish.1 = (f32[1,2,2,128]{3,2,1,0:T(2,128)}, f32[2,64,576]{2,1,0:T(8,128)}, f32[256,1024]{1,0:T(8,128)}) custom-call(f32[2,2,128]{2,1,0:T(2,128)} %get-tuple-element.6.holo_in, bf16[448,128]{1,0:T(8,128)(2,1)} %get-tuple-element.7.own_ref, bf16[320,128]{1,0:T(8,128)(2,1)} %get-tuple-element.8.other_ref, bf16[64,1024]{1,0:T(8,128)(2,1)} %bitcast.5), custom_call_target="tpu_custom_call" | custom-call | tf_op jit(solution)/shard_map/finish/pallas_call | solution.py:702

commit v5 on v4

--- a/solution.py
+++ b/solution.py
@@ -221,22 +221,6 @@
     def send_o(i):
         return remote(oout.at[i], oin.at[head], o_send.at[i], o_recv.at[head], source(i))
 
-    landed(0, 1 - c)
-    values(0, 0)
-
-    def first_block(i, carry):
-        @pl.when(i > 0)
-        def _():
-            remote(qin.at[i], qin.at[i], q_send.at[0], q_recv.at[i], mate).wait_recv()
-            top, bottom = unpack(qin[i])
-            qz[i, 0:HALF, :] = top
-            qz[i, HALF : 2 * HALF, :] = bottom
-
-        take(0, i, 0)
-        return carry
-
-    lax.fori_loop(0, 4, first_block, 0)
-
     def relay(blk):
         landed(blk, c)
         remote(
@@ -251,6 +235,28 @@
     def pass_on(blk):
         remote(kvb.at[blk, c], kvb.at[blk, c], c_send.at[blk], kv_recv.at[blk, c], mate).start()
 
+    landed(0, 1 - c)
+    values(0, 0)
+
+    def first_block(i, carry):
+        @pl.when(i > 0)
+        def _():
+            remote(qin.at[i], qin.at[i], q_send.at[0], q_recv.at[i], mate).wait_recv()
+            top, bottom = unpack(qin[i])
+            qz[i, 0:HALF, :] = top
+            qz[i, HALF : 2 * HALF, :] = bottom
+
+        take(0, i, 0)
+
+        @pl.when(i == 1)
+        def _():
+            landed(1, c)
+            pass_on(1)
+
+        return carry
+
+    lax.fori_loop(0, 4, first_block, 0)
+
     def middle(blk, carry):
         @pl.when(blk == 1)
         def _():
@@ -260,17 +266,21 @@
         def _():
             send_kv(3).start()
 
-        @pl.when(lax.rem(blk, 2) == 1)
-        def _():
-            landed(blk, c)
-            pass_on(blk)
-            relay(jnp.minimum(blk + 1, 6))
-
         landed(blk, 1 - c)
         values(blk, 0)
 
         def each(i, inner):
             take(blk, i, 0)
+
+            @pl.when(jnp.logical_and(lax.rem(blk, 2) == 1, i == 0))
+            def _():
+                relay(jnp.minimum(blk + 1, 6))
+
+            @pl.when(jnp.logical_and(lax.rem(blk, 2) == 0, i == 1))
+            def _():
+                landed(blk + 1, c)
+                pass_on(blk + 1)
+
             return inner
 
         lax.fori_loop(0, 4, each, 0)
@@ -278,11 +288,18 @@
 
     lax.fori_loop(1, 6, middle, 0)
 
+    landed(6, 1 - c)
+    values(6, 0)
+
+    def earlier(j, carry):
+        take(6, 3 - j, 0)
+        return carry
+
+    lax.fori_loop(0, 2, earlier, 0)
     landed(7, c)
     pass_on(7)
-    for blk in (6, 7):
-        landed(blk, 1 - c)
-        values(blk, blk - 6)
+    landed(7, 1 - c)
+    values(7, 1)
 
     def last_blocks(j, carry):
         i = 3 - j
@@ -291,7 +308,7 @@
             take(6 + k, i, k)
             return inner
 
-        lax.fori_loop(0, 2, each, 0)
+        lax.fori_loop(jnp.where(j < 2, 1, 0), 2, each, 0)
         whole = acc_ref[i]
         done = whole / pltpu.roll(whole, HEAD, 1)
         packed = jnp.where(low_h, pltpu.roll(done[0:HALF], HEAD, 1), done[HALF:])
@@ -423,11 +440,12 @@
     attention_part(ready, meanwhile, tok_ref, gain_ref, w_ref, ctx_ref, *attention_refs)
 
     ctx = ctx_ref[...]
-    pbuf[0] = dot_nt(w2_ref[0], ctx) + (dot_nt(w2_ref[1], ctx) + dot_nt(w2_ref[2], ctx))
+    share = dot_nt(w2_ref[0], ctx) + (dot_nt(w2_ref[1], ctx) + dot_nt(w2_ref[2], ctx))
+    pbuf[0] = share.astype(BF16)
     p_copy = remote(pbuf.at[0], pbuf.at[1], p_send.at[0], p_recv.at[0], to_mate)
     p_copy.start()
     p_copy.wait_recv()
-    ext[2] = (base_ref[...] + (pbuf[0] + pbuf[1])).astype(BF16)
+    ext[2] = (base_ref[...] + (pbuf[0].astype(F32) + pbuf[1].astype(F32))).astype(BF16)
     c_copy.wait_recv()
 
     halo = []
@@ -537,7 +555,8 @@
         source = lax.rem(t + k, n_t)
         return remote(chunk(buf, 0), rbuf.at[source], s1.at[k], r1.at[source], {"tok": source})
 
-    for k in range(1, n_t):
+    far_first = sorted(range(1, n_t), key=lambda k: -min(k, n_t - k))
+    for k in far_first:
         peer, item = phase1(k)
 
         @pl.when(peer < RS_CHUNKS)
@@ -552,7 +571,7 @@
         total = rbuf[0].astype(F32)
         for j in range(1, n_t):
             total = total + rbuf[j].astype(F32)
-        dbuf[dp] = total
+        dbuf[dp] = total.astype(BF16)
         for k in range(1, n_dp):
             peer = lax.rem(dp + k, n_dp)
             remote(dbuf.at[dp], dbuf.at[dp], s2.at[k], r2.at[dp], {"dp": peer}).start()
@@ -561,11 +580,11 @@
             remote(
                 dbuf.at[source], dbuf.at[source], s2.at[k], r2.at[source], {"dp": source}
             ).wait_recv()
-        whole = dbuf[0]
+        whole = dbuf[0].astype(F32)
         for j in range(1, n_dp):
-            whole = whole + dbuf[j]
+            whole = whole + dbuf[j].astype(F32)
         fbuf[pl.ds(pl.multiple_of(t * RS_ROWS, RS_ROWS), RS_ROWS), :] = whole.astype(BF16)
-        for k in range(1, n_t):
+        for k in far_first:
             peer = lax.rem(t + k, n_t)
             remote(chunk(fbuf, t), chunk(fbuf, t), s3.at[k], r3.at[t], {"tok": peer}).start()
 
@@ -636,7 +655,7 @@
             pltpu.VMEM((3, 64, local), BF16),
             pltpu.VMEM((64, rows), F32),
             pltpu.VMEM((2, 64, 576), BF16),
-            pltpu.VMEM((2, 64, 512), F32),
+            pltpu.VMEM((2, 64, 512), BF16),
             pltpu.VMEM((5, 64, 512), BF16),
             pltpu.VMEM((3, 2, 2, 2, 128), F32),
             pltpu.VMEM((576, 2048), BF16),
@@ -644,7 +663,7 @@
             pltpu.VMEM((576, 1024), BF16),
             pltpu.VMEM((448, 128), BF16),
             pltpu.VMEM((n_t, RS_ROWS, 128), BF16),
-            pltpu.VMEM((n_dp, RS_ROWS, 128), F32),
+            pltpu.VMEM((n_dp, RS_ROWS, 128), BF16),
             pltpu.VMEM((448, 128), BF16),
             pltpu.VMEM((320, 128), BF16),
             dma((2,)),

time: 90.5 us -> 88 us (0.972)
  Pallas kernels: 89.7 us -> 87.3 us
    pallas_call x1, Pallas kernels: 87.4 us -> 84.9 us  [step(): pl.pallas_call(step_kernel, out_shape=(jax.ShapeDtypeStruct(cot.shape, F3...]
where the time goes in v5:
time: 88 us; the launch traced here: 87.9 us
  Pallas kernels  87.3 us (99%)
    pallas_call x1, Pallas kernels, step(): pl.pallas_call(step_kernel, out_shape=(jax.ShapeDtypeStruct(cot.shape, F3...  84.9 us
    pallas_call x1, Pallas kernels, finish(): pl.pallas_call(finish_kernel, out_shape=(jax.ShapeDtypeStruct((1, *holo.s...  2.37 us

profile of v5, /device:TPU:1, one launch (start us, length us, event | category | flops | bytes accessed | tf_op | source)
XLA Modules:
  0.0 87.9 jit_solution(5709561082705382112)
XLA Ops:
  0.6 84.9 %step.1 = (f32[2,2,128]{2,1,0:T(2,128)}, bf16[448,128]{1,0:T(8,128)(2,1)}, bf16[320,128]{1,0:T(8,128)(2,1)}) custom-call(bf16[512,1024]{1,0:T(8,128)(2,1)} %bitcast.3, bf16[1024]{0:T(1024)(128)(2,1)} %gain_ref.1, bf16[3,1024,256]{2,1,0:T(8,128)(2,1)} %w_ref.1, bf16[256,1024]{1,0:T(8,128)(2,1)} %ow_ref.1, bf16[64,1024]{1,0:T(8,128)(2,1)} %bitcast.4, ...), custom_call_target="tpu_custom_call" | custom-call | tf_op jit(solution)/shard_map/step/pallas_call | solution.py:644
  85.5 2.4 %finish.1 = (f32[1,2,2,128]{3,2,1,0:T(2,128)}, f32[2,64,576]{2,1,0:T(8,128)}, f32[256,1024]{1,0:T(8,128)}) custom-call(f32[2,2,128]{2,1,0:T(2,128)} %get-tuple-element.6.holo_in, bf16[448,128]{1,0:T(8,128)(2,1)} %get-tuple-element.7.own_ref, bf16[320,128]{1,0:T(8,128)(2,1)} %get-tuple-element.8.other_ref, bf16[64,1024]{1,0:T(8,128)(2,1)} %bitcast.5), custom_call_target="tpu_custom_call" | custom-call | tf_op jit(solution)/shard_map/finish/pallas_call | solution.py:721

commit v6 on v5

--- a/solution.py
+++ b/solution.py
@@ -193,24 +193,26 @@
 
     place(0, qout[head])
 
+    def scores(blk, i):
+        return [dot_nt(qz[i], kvb[blk, half]) for half in range(2)]
+
+    def absorb(i, s, at_v):
+        m_old = m_ref[i]
+        top = jnp.maximum(
+            jnp.max(s[0], axis=1, keepdims=True), jnp.max(s[1], axis=1, keepdims=True)
+        )
+        m_new = jnp.maximum(m_old, top)
+        wide = jnp.concatenate([m_new] * (KT // 128), axis=1)
+        out = None
+        for half in range(2):
+            p = jnp.exp(s[half] - wide).astype(BF16)
+            o = dot_nn(p, vx[at_v, half])
+            out = o if out is None else out + o
+        acc_ref[i] = acc_ref[i] * jnp.exp(m_old - m_new) + out
+        m_ref[i] = m_new
+
     def take(blk, i, at_v):
-        for tile in range(2 * HALF // QT):
-            at = slice(tile * QT, (tile + 1) * QT)
-            q = qz[i, at, :]
-            s = [dot_nt(q, kvb[blk, half]) for half in range(2)]
-            m_old = m_ref[i, at, :]
-            top = jnp.maximum(
-                jnp.max(s[0], axis=1, keepdims=True), jnp.max(s[1], axis=1, keepdims=True)
-            )
-            m_new = jnp.maximum(m_old, top)
-            wide = jnp.concatenate([m_new] * (KT // 128), axis=1)
-            out = None
-            for half in range(2):
-                p = jnp.exp(s[half] - wide).astype(BF16)
-                o = dot_nn(p, vx[at_v, half])
-                out = o if out is None else out + o
-            acc_ref[i, at, :] = acc_ref[i, at, :] * jnp.exp(m_old - m_new) + out
-            m_ref[i, at, :] = m_new
+        absorb(i, scores(blk, i), at_v)
 
     def values(blk, at_v):
         low_k = low_lanes((KT, 128))
@@ -269,21 +271,25 @@
         landed(blk, 1 - c)
         values(blk, 0)
 
-        def each(i, inner):
-            take(blk, i, 0)
-
-            @pl.when(jnp.logical_and(lax.rem(blk, 2) == 1, i == 0))
-            def _():
-                relay(jnp.minimum(blk + 1, 6))
-
-            @pl.when(jnp.logical_and(lax.rem(blk, 2) == 0, i == 1))
-            def _():
-                landed(blk + 1, c)
-                pass_on(blk + 1)
-
-            return inner
-
-        lax.fori_loop(0, 4, each, 0)
+        ahead = scores(blk, 0)
+        for i in range(4):
+            now = ahead
+            if i < 3:
+                ahead = scores(blk, i + 1)
+            absorb(i, now, 0)
+            if i == 0:
+
+                @pl.when(lax.rem(blk, 2) == 1)
+                def _():
+                    relay(jnp.minimum(blk + 1, 6))
+
+            if i == 1:
+
+                @pl.when(lax.rem(blk, 2) == 0)
+                def _():
+                    landed(blk + 1, c)
+                    pass_on(blk + 1)
+
         return carry
 
     lax.fori_loop(1, 6, middle, 0)

time: 88 us -> 88 us (level)
  no operation moved by 1% of the time
where the time goes in v6:
time: 88 us; the launch traced here: 87.9 us
  Pallas kernels  87.3 us (99%)
    pallas_call x1, Pallas kernels, step(): pl.pallas_call(step_kernel, out_shape=(jax.ShapeDtypeStruct(cot.shape, F3...  84.9 us
    pallas_call x1, Pallas kernels, finish(): pl.pallas_call(finish_kernel, out_shape=(jax.ShapeDtypeStruct((1, *holo.s...  2.37 us

profile of v6, /device:TPU:1, one launch (start us, length us, event | category | flops | bytes accessed | tf_op | source)
XLA Modules:
  0.0 87.9 jit_solution(11470169130759204254)
XLA Ops:
  0.6 84.9 %step.1 = (f32[2,2,128]{2,1,0:T(2,128)}, bf16[448,128]{1,0:T(8,128)(2,1)}, bf16[320,128]{1,0:T(8,128)(2,1)}) custom-call(bf16[512,1024]{1,0:T(8,128)(2,1)} %bitcast.3, bf16[1024]{0:T(1024)(128)(2,1)} %gain_ref.1, bf16[3,1024,256]{2,1,0:T(8,128)(2,1)} %w_ref.1, bf16[256,1024]{1,0:T(8,128)(2,1)} %ow_ref.1, bf16[64,1024]{1,0:T(8,128)(2,1)} %bitcast.4, ...), custom_call_target="tpu_custom_call" | custom-call | tf_op jit(solution)/shard_map/step/pallas_call | solution.py:650
  85.5 2.4 %finish.1 = (f32[1,2,2,128]{3,2,1,0:T(2,128)}, f32[2,64,576]{2,1,0:T(8,128)}, f32[256,1024]{1,0:T(8,128)}) custom-call(f32[2,2,128]{2,1,0:T(2,128)} %get-tuple-element.6.holo_in, bf16[448,128]{1,0:T(8,128)(2,1)} %get-tuple-element.7.own_ref, bf16[320,128]{1,0:T(8,128)(2,1)} %get-tuple-element.8.other_ref, bf16[64,1024]{1,0:T(8,128)(2,1)} %bitcast.5), custom_call_target="tpu_custom_call" | custom-call | tf_op jit(solution)/shard_map/finish/pallas_call | solution.py:727

commit v7 on v6

--- a/solution.py
+++ b/solution.py
@@ -455,12 +455,13 @@
     c_copy.wait_recv()
 
     halo = []
-    for k, (off, slot) in enumerate(((1, 1), (-1, 3), (2, 0), (-2, 4))):
+    for k, (off, slot) in enumerate(((-1, 3), (2, 0), (1, 1), (-2, 4))):
         peer = {"tok": lax.rem(t + off + n_t, n_t)}
         halo.append(remote(ext.at[2], ext.at[slot], h_send.at[k], h_recv.at[k], peer))
-        if k < 2:
+        if abs(off) == 1:
+            at = 1 - (off + 1) // 2
             halo.append(
-                remote(cbuf.at[1], cbuf.at[2 * k], h_send.at[4 + k], h_recv.at[4 + k], peer)
+                remote(cbuf.at[1], cbuf.at[2 * at], h_send.at[4 + at], h_recv.at[4 + at], peer)
             )
     for item in halo:
         item.start()

time: 88 us -> 88.1 us (level)
  no operation moved by 1% of the time
where the time goes in v7:
time: 88.1 us; the launch traced here: 87.8 us
  Pallas kernels  87.1 us (99%)
    pallas_call x1, Pallas kernels, step(): pl.pallas_call(step_kernel, out_shape=(jax.ShapeDtypeStruct(cot.shape, F3...  84.8 us
    pallas_call x1, Pallas kernels, finish(): pl.pallas_call(finish_kernel, out_shape=(jax.ShapeDtypeStruct((1, *holo.s...  2.37 us

profile of v7, /device:TPU:1, one launch (start us, length us, event | category | flops | bytes accessed | tf_op | source)
XLA Modules:
  0.0 87.8 jit_solution(11739768751629537659)
XLA Ops:
  0.6 84.8 %step.1 = (f32[2,2,128]{2,1,0:T(2,128)}, bf16[448,128]{1,0:T(8,128)(2,1)}, bf16[320,128]{1,0:T(8,128)(2,1)}) custom-call(bf16[512,1024]{1,0:T(8,128)(2,1)} %bitcast.3, bf16[1024]{0:T(1024)(128)(2,1)} %gain_ref.1, bf16[3,1024,256]{2,1,0:T(8,128)(2,1)} %w_ref.1, bf16[256,1024]{1,0:T(8,128)(2,1)} %ow_ref.1, bf16[64,1024]{1,0:T(8,128)(2,1)} %bitcast.4, ...), custom_call_target="tpu_custom_call" | custom-call | tf_op jit(solution)/shard_map/step/pallas_call | solution.py:651
  85.4 2.4 %finish.1 = (f32[1,2,2,128]{3,2,1,0:T(2,128)}, f32[2,64,576]{2,1,0:T(8,128)}, f32[256,1024]{1,0:T(8,128)}) custom-call(f32[2,2,128]{2,1,0:T(2,128)} %get-tuple-element.6.holo_in, bf16[448,128]{1,0:T(8,128)(2,1)} %get-tuple-element.7.own_ref, bf16[320,128]{1,0:T(8,128)(2,1)} %get-tuple-element.8.other_ref, bf16[64,1024]{1,0:T(8,128)(2,1)} %bitcast.5), custom_call_target="tpu_custom_call" | custom-call | tf_op jit(solution)/shard_map/finish/pallas_call | solution.py:728
